TPU v7x, 256 devices: a whole 4x4x8 slice. The times are simulated.
256 devices in a mesh: space: 16 (over z, core), vel: 16 (over x, y).
Axes of the slice: x: 4, y: 4, z: 8, core: 2. Of those that a mesh axis runs over, the one named last changes fastest.
Arguments:
- distribution: float32 [1024, 32768], P('space', 'vel'), may hold values from 0.05 to 2
- collision_order: int32 [16, 64], P('space'), may hold values from 0 to 63, each once within a row
- collision_blocks: int32 [16], P('space'), may hold values from 1 to 4, 32 in all
- kernels: float32 [5, 32768], replicated, may hold values from -6 to 6
Outputs:
- new_distribution: float32 [1024, 32768], P('space', 'vel')
Inputs may be any that keep to these rules, and one draw needn't show every extreme that they name: `collision_order`: each row is an ordering of the 64 local cells. `collision_blocks`: the counts sum to 32, which is 2 on average for each index of space, and the largest is 4.
All inputs are finite; a program needn't handle non-finite values. No bound on the sum of `collision_blocks` on one device may be relied on, other than what follows from the above.
Results may differ from a plain program's by a relative error of at most 0.0001.
Values sent between devices are 32-bit elements; how exact they have to be, the bound alone decides.
No kernel may reach another device: no remote copies, remote signals or barrier semaphores. Data moves between devices by JAX's collectives and lax.ppermute only.
A program may use at most 64 MiB of HBM per device.

v0:
```python
import functools
import math

import jax
import jax.numpy as jnp
import numpy as np
from jax import lax
from jax.experimental import pallas as pl
from jax.experimental.pallas import tpu as pltpu
from jax.sharding import Mesh
from jax.sharding import PartitionSpec as P

NV = 32
BLOCK_CELLS = 16
KERN = 5
VEL = ("vel_0", "vel_1")
COURANT_MAX = 0.95
STEP_SCALE = 0.25
F32 = jnp.float32
BF16 = jnp.bfloat16


def small_tables():
    lane = np.arange(128)
    y4, z = lane // 32, lane % 32
    base = (8 * np.outer(y4, y4) + np.outer(z, z)) % 32
    row = np.arange(512)
    v, x2, ch = row // 32, (row % 16) // 8, row % 8
    x = 2 * v + x2
    left = np.outer(np.arange(32), x) % 32
    turn = (4 * np.outer(np.arange(8), ch)) % 32
    tables = []
    for phase in (base, left, turn):
        angle = phase * (2.0 * math.pi / 32)
        tables += [np.cos(angle).astype(np.float32), np.sin(angle).astype(np.float32)]
    neg = (32 - z) % 32
    flips = []
    for other in ((4 - y4) % 4, 3 - y4):
        flip = np.zeros((128, 128), np.float32)
        flip[other * 32 + neg, lane] = 1.0
        flips.append(flip)
    tables.append(np.stack(flips))
    return tables


def split(a):
    hi = a.astype(BF16)
    lo = (a - hi.astype(F32)).astype(BF16)
    return hi, lo


def dot(a, b):
    return jnp.dot(a, b, preferred_element_type=F32)


def dot3(ahi, alo, bhi, blo):
    return dot(ahi, bhi) + dot(ahi, blo) + dot(alo, bhi)


def transport_kernel(side_ref, courant_ref, dist_ref, halo_ref, out_ref, raw):
    step = side_ref[0]
    zero = jnp.zeros((32, 128), F32)
    raw[0:32, :] = zero
    raw[66 * 16 : 68 * 16, :] = zero
    for tile in range(8):
        for j in range(16):
            raw[pl.ds((8 * tile + 2) * 16 + j, 8, stride=16), :] = dist_ref[
                8 * tile : 8 * tile + 8, 128 * j : 128 * j + 128
            ]
    at = pl.multiple_of(jnp.where(step < 0, 0, 66 * 16), 16)
    for j in range(16):
        raw[pl.ds(at + j, 2, stride=16), :] = halo_ref[:, 128 * j : 128 * j + 128]
    for cell in range(64):
        for half in range(2):
            a = courant_ref[half]
            here = (cell + 2) * 16 + 8 * half
            f0 = raw[pl.ds(here, 8), :]
            f1 = raw[pl.ds(pl.multiple_of(here + 16 * step, 8), 8), :]
            f2 = raw[pl.ds(pl.multiple_of(here + 32 * step, 8), 8), :]
            once = f0 - a * (f0 - f1)
            beside = f1 - a * (f1 - f2)
            out_ref[cell // 4, (cell % 4) * 16 + 8 * half : (cell % 4) * 16 + 8 * half + 8, :] = (
                once - a * (once - beside)
            )


def tables_kernel(
    where_ref, order_ref, kern_ref, c0_ref, s0_ref, cl_ref, sl_ref, ct_ref, st_ref, flip_ref,
    lhi_ref, llo_ref, ihi_ref, ilo_ref, whi_ref, wlo_ref, vhi_ref, vlo_ref, ks_ref, mask_ref,
    rows, turned, full,
):
    position = lax.broadcasted_iota(jnp.int32, (1, 64), 1)
    first = position < BLOCK_CELLS * where_ref[1]
    for c in range(4):
        hit = jnp.where(first & (order_ref[...] == 4 * where_ref[0] + c), STEP_SCALE, 0.0)
        mask_ref[16 * c : 16 * c + 16, :] = jnp.broadcast_to(
            jnp.sum(hit, axis=1, keepdims=True), (16, 128)
        )
    c0, s0 = c0_ref[...], s0_ref[...]
    lane_y4 = lax.broadcasted_iota(jnp.int32, (1, 128), 1) // 32
    for k8 in range(8):
        cosv = [math.cos(2 * math.pi * y4 * k8 / 32) for y4 in range(4)]
        sinv = [math.sin(2 * math.pi * y4 * k8 / 32) for y4 in range(4)]
        for y4 in range(4):
            part = slice(32 * y4, 32 * y4 + 32)
            lower = slice(128 + 32 * y4, 160 + 32 * y4)
            c = cosv[y4] * c0[part] - sinv[y4] * s0[part]
            s = cosv[y4] * s0[part] + sinv[y4] * c0[part]
            chi, clo = split(c)
            shi, slo = split(s)
            for ref, cc, ss in ((whi_ref, chi, shi), (wlo_ref, clo, slo)):
                ref[k8, part, 0:128] = cc
                ref[k8, part, 128:256] = -ss
                ref[k8, lower, 0:128] = ss
                ref[k8, lower, 128:256] = cc
        cvec = jnp.full((1, 128), cosv[0], F32)
        svec = jnp.full((1, 128), sinv[0], F32)
        for y4 in range(1, 4):
            cvec = jnp.where(lane_y4 == y4, cosv[y4], cvec)
            svec = jnp.where(lane_y4 == y4, sinv[y4], svec)
        c = cvec * c0 - svec * s0
        s = cvec * s0 + svec * c0
        chi, clo = split(c)
        shi, slo = split(s)
        for ref, cc, ss in ((vhi_ref, chi, shi), (vlo_ref, clo, slo)):
            ref[k8, 0:128, 0:128] = cc
            ref[k8, 0:128, 128:256] = ss
            ref[k8, 128:256, 0:128] = -ss
            ref[k8, 128:256, 128:256] = cc
    cl, sl = cl_ref[...], sl_ref[...]
    is_real = (lax.broadcasted_iota(jnp.int32, (1, 512), 1) // 16) % 2 == 0
    for k8 in range(8):
        ct, st = ct_ref[k8 : k8 + 1, :], st_ref[k8 : k8 + 1, :]
        c = ct * cl - st * sl
        s = ct * sl + st * cl
        full[64 * k8 : 64 * k8 + 32, :] = jnp.where(is_real, c, s)
        full[64 * k8 + 32 : 64 * k8 + 64, :] = jnp.where(is_real, -s, c)
    for i in range(4):
        part = slice(128 * i, 128 * i + 128)
        lhi_ref[part, :], llo_ref[part, :] = split(full[part, :])
        ihi_ref[part, :], ilo_ref[part, :] = split(full[:, part].T)
    for kx in range(32):
        for ch in range(8):
            at = kx * 8 + ch
            back = ((32 - kx) % 32) * 8 + ch
            tile = kern_ref[:, at * 128 : at * 128 + 128]
            rows[pl.ds(at, KERN, stride=256), :] = tile
            turned[pl.ds(back, KERN, stride=256), :] = tile
    group = lax.broadcasted_iota(jnp.int32, (32, 128), 1) // 32

    def ordered(src, t, k8):
        g, h = k8 % 4, k8 // 4
        out = None
        for k4 in range(4):
            piece = src[pl.ds(t * 256 + 2 * k4 + h, 32, stride=8), :]
            if k4 != g:
                piece = pltpu.roll(piece, ((k4 - g) % 4) * 32, 1)
            out = piece if out is None else jnp.where(group == k4, piece, out)
        return out

    scale = 0.5 / NV**3
    for k8 in range(8):
        flip = flip_ref[0 if k8 == 0 else 1].astype(BF16)
        for t in range(KERN):
            straight = ordered(rows, t, k8)
            other = ordered(turned, t, (8 - k8) % 8)
            hi, lo = split(other)
            mirrored = dot(hi, flip) + dot(lo, flip)
            ks_ref[k8, t] = scale * (straight + mirrored)


def collide_kernel(
    x_ref, lhi_ref, llo_ref, ihi_ref, ilo_ref, whi_ref, wlo_ref, vhi_ref, vlo_ref, ks_ref, mask_ref,
    out_ref, y, bhi, blo, acc,
):
    def cells(p):
        return x_ref[:, 32 * p : 32 * p + 32, :].reshape(512, 128)

    xhi, xlo = split(jnp.concatenate([cells(0), cells(1)], axis=1))
    y[...] = dot3(lhi_ref[...], llo_ref[...], xhi, xlo)
    for k8 in range(8):
        top = slice(64 * k8, 64 * k8 + 32)
        low = slice(64 * k8 + 32, 64 * k8 + 64)
        field = jnp.concatenate(
            [
                jnp.concatenate([y[top, 0:128], y[low, 0:128]], axis=1),
                jnp.concatenate([y[top, 128:256], y[low, 128:256]], axis=1),
            ],
            axis=0,
        )
        fhi, flo = split(field)
        spectrum = dot3(fhi, flo, whi_ref[k8], wlo_ref[k8])
        parts = []
        for t in range(KERN):
            ks = ks_ref[k8, t]
            ks = jnp.concatenate([ks, ks], axis=1)
            parts += [spectrum[0:32] * ks, spectrum[32:64] * ks]
        ghi, glo = split(jnp.concatenate(parts, axis=0))
        back = dot3(ghi, glo, vhi_ref[k8], vlo_ref[k8])
        hi, lo = split(back)
        for n in range(2 * KERN):
            for ref, val in ((bhi, hi), (blo, lo)):
                ref[top, 128 * n : 128 * n + 128] = val[32 * n : 32 * n + 32, 0:128]
                ref[low, 128 * n : 128 * n + 128] = val[32 * n : 32 * n + 32, 128:256]

    def part(t):
        cols = slice(256 * t, 256 * t + 256)
        return dot3(ihi_ref[...], ilo_ref[...], bhi[:, cols], blo[:, cols])

    acc[...] = part(0)
    acc[...] = acc[...] * part(1)
    y[...] = part(2)
    acc[...] = acc[...] + y[...] * part(3)
    y[...] = part(4)
    for p in range(2):
        lanes = slice(128 * p, 128 * p + 128)
        mask = mask_ref[32 * p : 32 * p + 32, :]
        for v in range(16):
            part_rows = slice(32 * v, 32 * v + 32)
            f = x_ref[v, 32 * p : 32 * p + 32, :]
            out_ref[v, 32 * p : 32 * p + 32, :] = f + mask * (
                acc[part_rows, lanes] - f * y[part_rows, lanes]
            )


def place_kernel(in_ref, out_ref):
    for tile in range(8):
        for j in range(16):
            out_ref[8 * tile : 8 * tile + 8, 128 * j : 128 * j + 128] = in_ref[
                pl.ds(tile * 128 + j, 8, stride=16), :
            ]


VM = pl.BlockSpec(memory_space=pltpu.VMEM)
SM = pl.BlockSpec(memory_space=pltpu.SMEM)


def shape(*dims, dtype=F32):
    return jax.ShapeDtypeStruct(dims, dtype)


def params(mib):
    return pltpu.CompilerParams(vmem_limit_bytes=mib << 20)


def transport(side, courant, dist, halo):
    return pl.pallas_call(
        transport_kernel,
        out_shape=shape(16, 64, 128),
        in_specs=[SM, SM, VM, VM],
        out_specs=VM,
        scratch_shapes=[pltpu.VMEM((68 * 16, 128), F32)],
        compiler_params=params(8),
        name="transport",
    )(side, courant, dist, halo)


def make_tables(where, order, kernels):
    tables = small_tables()
    half = shape(512, 512, dtype=BF16)
    eight = shape(8, 256, 256, dtype=BF16)
    return pl.pallas_call(
        tables_kernel,
        out_shape=[half] * 4 + [eight] * 4 + [shape(8, KERN, 32, 128), shape(64, 128)],
        in_specs=[SM] + [VM] * 9,
        out_specs=[VM] * 10,
        scratch_shapes=[
            pltpu.VMEM((KERN * 256, 128), F32),
            pltpu.VMEM((KERN * 256, 128), F32),
            pltpu.VMEM((512, 512), F32),
        ],
        compiler_params=params(20),
        name="tables",
    )(where, order, kernels, *[jnp.asarray(t) for t in tables])


def collide(x, tables):
    return pl.pallas_call(
        collide_kernel,
        out_shape=shape(16, 64, 128),
        in_specs=[VM] * 11,
        out_specs=VM,
        scratch_shapes=[
            pltpu.VMEM((512, 256), F32),
            pltpu.VMEM((512, 1280), BF16),
            pltpu.VMEM((512, 1280), BF16),
            pltpu.VMEM((512, 256), F32),
        ],
        compiler_params=params(24),
        name="collide",
    )(x, *tables)


def place(x):
    return pl.pallas_call(
        place_kernel,
        out_shape=shape(64, 2048),
        in_specs=[VM],
        out_specs=VM,
        compiler_params=params(8),
        name="place",
    )(x.reshape(1024, 128))


def local(distribution, collision_order, collision_blocks, kernels):
    v = lax.axis_index(VEL)
    rising = v >= 8
    x = 2 * v + lax.iota(jnp.int32, 2)
    courant = jnp.abs(COURANT_MAX * (2.0 * x.astype(F32) - (NV - 1)) / (NV - 1))
    side = jnp.where(rising, -1, 1).astype(jnp.int32)[None]
    edge = jnp.where(rising, distribution[62:64], distribution[0:2])
    pairs = []
    for s in range(16):
        for u in range(16):
            to = s + 1 if u >= 8 else s - 1
            if 0 <= to < 16:
                pairs.append((s * 16 + u, to * 16 + u))
    halo = lax.ppermute(edge, ("space",) + VEL, pairs)
    where = jnp.stack([v.astype(jnp.int32), collision_blocks[0]])
    tables = make_tables(where, collision_order, kernels)
    mine = transport(side, courant, distribution, halo)
    cells = lax.all_to_all(mine, VEL, split_axis=0, concat_axis=0, tiled=True)
    done = collide(cells, tables)
    back = lax.all_to_all(done, VEL, split_axis=0, concat_axis=0, tiled=True)
    return place(back)


def solution(mesh):
    finer = Mesh(mesh.devices.reshape(mesh.shape["space"], 4, 4), ("space", "vel_0", "vel_1"))
    in_specs = (P("space", VEL), P("space", None), P("space"), P())
    out_specs = P("space", VEL)
    return jax.shard_map(local, mesh=finer, in_specs=in_specs, out_specs=out_specs, check_vma=False)
```

profile of v0, /device:TPU:96, one launch (start us, length us, event | category | flops | bytes accessed | tf_op | source)
XLA Modules:
  0.0 62.8 jit_solution(12763835760114189474)
XLA Ops:
  0.0 0.9 %slice_select_fusion = f32[2,2048]{1,0:T(2,128)S(1)} fusion(f32[64,2048]{1,0:T(8,128)} %dist_ref.1, pred[]{:T(512)S(6)} %ge.3), kind=kLoop, calls=%fused_computation | loop fusion | flops 4096 | bytes 49153 | tf_op jit(solution)/shard_map/jit(_where)/select_n | solution.py:311
  0.9 1.9 %collective-permute-start = (f32[2,2048]{1,0:T(2,128)S(1)}, f32[2,2048]{1,0:T(2,128)S(1)}, u32[]{:S(2)}, u32[]{:S(2)}) collective-permute-start(f32[2,2048]{1,0:T(2,128)S(1)} %slice_select_fusion), channel_id=1, source_target_pairs={{8,24},{9,25},{10,26},{11,27},{12,28},{13,29},{14,30},{15,31},{16,... | collective-permute-start | bytes 49160 | tf_op jit(solution)/shard_map/ppermute | solution.py:318
  2.8 1.4 %collective-permute-done.halo_ref = f32[2,2048]{1,0:T(2,128)S(1)} collective-permute-done((f32[2,2048]{1,0:T(2,128)S(1)}, f32[2,2048]{1,0:T(2,128)S(1)}, u32[]{:S(2)}, u32[]{:S(2)}) %collective-permute-start) | collective-permute-done | bytes 16416 | tf_op jit(solution)/shard_map/ppermute | solution.py:318
  4.2 0.0 copy-start.5
  4.2 1.0 %copy-done.5 = f32[64,2048]{1,0:T(8,128)S(1)} copy-done((f32[64,2048]{1,0:T(8,128)S(1)}, f32[64,2048]{1,0:T(8,128)}, u32[]{:S(2)}) %copy-start.5) | copy-done | bytes 524312
  5.3 1.7 %transport.1 = f32[16,64,128]{2,1,0:T(8,128)} custom-call(s32[1]{0:T(128)} %bitcast.side_ref, f32[2]{0:T(128)S(1)} %multiply_abs_fusion.courant_ref, f32[64,2048]{1,0:T(8,128)S(1)} %copy-done.5, f32[2,2048]{1,0:T(2,128)S(1)} %collective-permute-done.halo_ref), custom_call_target="tpu_custom_call" | custom-call | tf_op jit(solution)/shard_map/transport/pallas_call | solution.py:247
  6.9 0.0 copy-start.14
  6.9 0.0 copy-start.15
  6.9 0.0 copy-start.16
  6.9 0.0 copy-start.21
  6.9 8.9 %all-to-all-start = ((f32[16,64,128]{2,1,0:T(8,128)}), f32[16,64,128]{2,1,0:T(8,128)S(1)}, u32[]{:S(2)}, u32[]{:S(2)}) async-start(f32[16,64,128]{2,1,0:T(8,128)} %transport.1), calls=%async_computation | async-start | bytes 1048576 | tf_op jit(solution)/shard_map/all_to_all | solution.py:322
  16.5 0.0 copy-start.23
  16.5 0.1 pad_add_fusion.where_ref
  16.6 0.0 copy-done.14
  16.6 0.0 copy-done.15
  16.6 0.0 copy-done.16
  16.6 0.0 copy-done.21
  16.6 0.6 copy-done.23
  17.2 0.0 copy-start.4
  17.2 1.2 %copy-done.4 = f32[5,32768]{1,0:T(8,128)S(1)} copy-done((f32[5,32768]{1,0:T(8,128)S(1)}, f32[5,32768]{1,0:T(8,128)}, u32[]{:S(2)}) %copy-start.4) | copy-done | bytes 655384
  18.4 0.0 copy-start.17
  18.4 0.8 %copy-done.17 = f32[128,128]{1,0:T(8,128)S(1)} copy-done((f32[128,128]{1,0:T(8,128)S(1)}, f32[128,128]{1,0:T(8,128)}, u32[]{:S(2)}) %copy-start.17) | copy-done | bytes 65560
  19.2 0.0 copy-start.18
  19.2 0.8 %copy-done.18 = f32[128,128]{1,0:T(8,128)S(1)} copy-done((f32[128,128]{1,0:T(8,128)S(1)}, f32[128,128]{1,0:T(8,128)}, u32[]{:S(2)}) %copy-start.18) | copy-done | bytes 65560
  20.1 0.0 copy-start.22
  20.1 0.7 %copy-done.22 = f32[8,512]{1,0:T(8,128)S(1)} copy-done((f32[8,512]{1,0:T(8,128)S(1)}, f32[8,512]{1,0:T(8,128)}, u32[]{:S(2)}) %copy-start.22) | copy-done | bytes 16408
  20.8 3.5 %tables.1 = (bf16[512,512]{1,0:T(8,128)(2,1)S(1)}, bf16[512,512]{1,0:T(8,128)(2,1)S(1)}, bf16[512,512]{1,0:T(8,128)(2,1)S(1)}, bf16[512,512]{1,0:T(8,128)(2,1)S(...) custom-call(s32[2]{0:T(128)S(1)} %pad_add_fusion.where_ref, ...), custom_call_target="tpu_custom_call" | custom-call | tf_op jit(solution)/shard_map/tables/pallas_call | solution.py:262
  24.3 0.0 copy-start
  24.3 1.0 %copy-done = bf16[8,256,256]{2,1,0:T(8,128)(2,1)} copy-done((bf16[8,256,256]{2,1,0:T(8,128)(2,1)}, bf16[8,256,256]{2,1,0:T(8,128)(2,1)S(1)}, u32[]{:S(2)}) %copy-start) | copy-done | bytes 1048600
  25.3 0.0 copy-start.2
  25.3 0.9 %copy-done.2 = bf16[8,256,256]{2,1,0:T(8,128)(2,1)} copy-done((bf16[8,256,256]{2,1,0:T(8,128)(2,1)}, bf16[8,256,256]{2,1,0:T(8,128)(2,1)S(1)}, u32[]{:S(2)}) %copy-start.2) | copy-done | bytes 1048600
  26.2 0.0 copy-start.6
  26.2 0.8 %copy-done.6 = bf16[512,512]{1,0:T(8,128)(2,1)} copy-done((bf16[512,512]{1,0:T(8,128)(2,1)}, bf16[512,512]{1,0:T(8,128)(2,1)S(1)}, u32[]{:S(2)}) %copy-start.6) | copy-done | bytes 524312
  27.0 0.8 %copy-done.8 = bf16[512,512]{1,0:T(8,128)(2,1)} copy-done((bf16[512,512]{1,0:T(8,128)(2,1)}, bf16[512,512]{1,0:T(8,128)(2,1)S(1)}, u32[]{:S(2)}) %copy-start.8) | copy-done | bytes 524312
  27.8 0.8 %copy-done.10 = bf16[512,512]{1,0:T(8,128)(2,1)} copy-done((bf16[512,512]{1,0:T(8,128)(2,1)}, bf16[512,512]{1,0:T(8,128)(2,1)S(1)}, u32[]{:S(2)}) %copy-start.10) | copy-done | bytes 524312
  28.6 0.8 %copy-done.12 = bf16[512,512]{1,0:T(8,128)(2,1)} copy-done((bf16[512,512]{1,0:T(8,128)(2,1)}, bf16[512,512]{1,0:T(8,128)(2,1)S(1)}, u32[]{:S(2)}) %copy-start.12) | copy-done | bytes 524312
  29.4 0.6 copy-done.19
  30.0 0.0 all-to-all-done.x_ref
  30.0 1.2 %copy-done.1 = bf16[8,256,256]{2,1,0:T(8,128)(2,1)S(1)} copy-done((bf16[8,256,256]{2,1,0:T(8,128)(2,1)S(1)}, bf16[8,256,256]{2,1,0:T(8,128)(2,1)}, u32[]{:S(2)}) %copy-start.1) | copy-done | bytes 1048600
  31.3 1.2 %copy-done.3 = bf16[8,256,256]{2,1,0:T(8,128)(2,1)S(1)} copy-done((bf16[8,256,256]{2,1,0:T(8,128)(2,1)S(1)}, bf16[8,256,256]{2,1,0:T(8,128)(2,1)}, u32[]{:S(2)}) %copy-start.3) | copy-done | bytes 1048600
  32.5 1.0 %copy-done.7 = bf16[512,512]{1,0:T(8,128)(2,1)S(1)} copy-done((bf16[512,512]{1,0:T(8,128)(2,1)S(1)}, bf16[512,512]{1,0:T(8,128)(2,1)}, u32[]{:S(2)}) %copy-start.7) | copy-done | bytes 524312
  33.5 1.0 %copy-done.9 = bf16[512,512]{1,0:T(8,128)(2,1)S(1)} copy-done((bf16[512,512]{1,0:T(8,128)(2,1)S(1)}, bf16[512,512]{1,0:T(8,128)(2,1)}, u32[]{:S(2)}) %copy-start.9) | copy-done | bytes 524312
  34.6 1.0 %copy-done.11 = bf16[512,512]{1,0:T(8,128)(2,1)S(1)} copy-done((bf16[512,512]{1,0:T(8,128)(2,1)S(1)}, bf16[512,512]{1,0:T(8,128)(2,1)}, u32[]{:S(2)}) %copy-start.11) | copy-done | bytes 524312
  35.6 1.0 %copy-done.13 = bf16[512,512]{1,0:T(8,128)(2,1)S(1)} copy-done((bf16[512,512]{1,0:T(8,128)(2,1)S(1)}, bf16[512,512]{1,0:T(8,128)(2,1)}, u32[]{:S(2)}) %copy-start.13) | copy-done | bytes 524312
  36.6 0.8 %copy-done.20 = f32[64,128]{1,0:T(8,128)S(1)} copy-done((f32[64,128]{1,0:T(8,128)S(1)}, f32[64,128]{1,0:T(8,128)}, u32[]{:S(2)}) %copy-start.20) | copy-done | bytes 32792
  37.4 5.4 %collide.1 = f32[16,64,128]{2,1,0:T(8,128)S(1)} custom-call(f32[16,64,128]{2,1,0:T(8,128)S(1)} %all-to-all-done.x_ref, bf16[512,512]{1,0:T(8,128)(2,1)S(1)} %copy-done.7, bf16[512,512]{1,0:T(8,128)(2,1)S(1)} %copy-done.9, bf16[512,512]{1,0:T(8,128)(2,1)S(1)} %copy-done.11, bf16[512,512]{1,0:T(8,128)(2,1)S(1)} %copy-done.13, ...), custom_call_target="tpu_custom_call" | custom-call | tf_op jit(solution)/shard_map/collide/pallas_call | solution.py:278
  42.8 19.1 %all_to_all.10 = f32[16,64,128]{2,1,0:T(8,128)S(1)} all-to-all(f32[16,64,128]{2,1,0:T(8,128)S(1)} %collide.1), channel_id=1, replica_groups=mesh['space'=16,'vel_0'=4,'vel_1'=4] {'vel_0','vel_1'}, dimensions={0} | all-to-all | bytes 1048576 | tf_op jit(solution)/shard_map/all_to_all | solution.py:324
  61.9 1.0 %place.1 = f32[64,2048]{1,0:T(8,128)} custom-call(f32[1024,128]{1,0:T(8,128)S(1)} %bitcast.3), custom_call_target="tpu_custom_call" | custom-call | tf_op jit(solution)/shard_map/place/pallas_call | solution.py:295
  (12 shorter events, 0.0 us)
Async XLA Ops:
  0.9 3.4 %collective-permute-start = (f32[2,2048]{1,0:T(2,128)S(1)}, f32[2,2048]{1,0:T(2,128)S(1)}, u32[]{:S(2)}, u32[]{:S(2)}) collective-permute-start(f32[2,2048]{1,0:T(2,128)S(1)} %slice_select_fusion), channel_id=1, source_target_pairs={{8,24},{9,25},{10,26},{11,27},{12,28},{13,29},{14,30},{15,31},{16,... | collective-permute-start | bytes 49160 | tf_op jit(solution)/shard_map/ppermute | solution.py:318
  4.2 1.0 %copy-start.5 = (f32[64,2048]{1,0:T(8,128)S(1)}, f32[64,2048]{1,0:T(8,128)}, u32[]{:S(2)}) copy-start(f32[64,2048]{1,0:T(8,128)} %dist_ref.1) | copy-start | bytes 1572868
  6.9 9.6 %copy-start.14 = (f32[2,128,128]{2,1,0:T(8,128)S(1)}, f32[2,128,128]{2,1,0:T(8,128)}, u32[]{:S(2)}) copy-start(f32[2,128,128]{2,1,0:T(8,128)} %constant.46.clone.flip_ref) | copy-start | bytes 393220
  6.9 9.6 %copy-start.15 = (f32[32,512]{1,0:T(8,128)S(1)}, f32[32,512]{1,0:T(8,128)}, u32[]{:S(2)}) copy-start(f32[32,512]{1,0:T(8,128)} %constant.43.clone.sl_ref) | copy-start | bytes 196612
  6.9 9.6 %copy-start.16 = (f32[32,512]{1,0:T(8,128)S(1)}, f32[32,512]{1,0:T(8,128)}, u32[]{:S(2)}) copy-start(f32[32,512]{1,0:T(8,128)} %constant.42.clone.cl_ref) | copy-start | bytes 196612
  6.9 9.6 %copy-start.21 = (f32[8,512]{1,0:T(8,128)S(1)}, f32[8,512]{1,0:T(8,128)}, u32[]{:S(2)}) copy-start(f32[8,512]{1,0:T(8,128)} %constant.45.clone.st_ref) | copy-start | bytes 49156
  6.9 23.1 %all-to-all-start = ((f32[16,64,128]{2,1,0:T(8,128)}), f32[16,64,128]{2,1,0:T(8,128)S(1)}, u32[]{:S(2)}, u32[]{:S(2)}) async-start(f32[16,64,128]{2,1,0:T(8,128)} %transport.1), calls=%async_computation | async-start | bytes 1048576 | tf_op jit(solution)/shard_map/all_to_all | solution.py:322
  16.5 0.7 %copy-start.23 = (s32[1,64]{1,0:T(1,128)S(1)}, s32[1,64]{1,0:T(1,128)}, u32[]{:S(2)}) copy-start(s32[1,64]{1,0:T(1,128)} %order_ref.1) | copy-start | bytes 772
  17.2 1.2 %copy-start.4 = (f32[5,32768]{1,0:T(8,128)S(1)}, f32[5,32768]{1,0:T(8,128)}, u32[]{:S(2)}) copy-start(f32[5,32768]{1,0:T(8,128)} %kern_ref.1) | copy-start | bytes 1966084
  18.4 0.8 %copy-start.17 = (f32[128,128]{1,0:T(8,128)S(1)}, f32[128,128]{1,0:T(8,128)}, u32[]{:S(2)}) copy-start(f32[128,128]{1,0:T(8,128)} %constant.41.clone.s0_ref) | copy-start | bytes 196612
  19.2 0.8 %copy-start.18 = (f32[128,128]{1,0:T(8,128)S(1)}, f32[128,128]{1,0:T(8,128)}, u32[]{:S(2)}) copy-start(f32[128,128]{1,0:T(8,128)} %constant.40.clone.c0_ref) | copy-start | bytes 196612
  20.1 0.7 %copy-start.22 = (f32[8,512]{1,0:T(8,128)S(1)}, f32[8,512]{1,0:T(8,128)}, u32[]{:S(2)}) copy-start(f32[8,512]{1,0:T(8,128)} %constant.44.clone.ct_ref) | copy-start | bytes 49156
  24.3 1.0 %copy-start = (bf16[8,256,256]{2,1,0:T(8,128)(2,1)}, bf16[8,256,256]{2,1,0:T(8,128)(2,1)S(1)}, u32[]{:S(2)}) copy-start(bf16[8,256,256]{2,1,0:T(8,128)(2,1)S(1)} %get-tuple-element.21.vhi_ref) | copy-start | bytes 3145732
  25.3 0.9 %copy-start.2 = (bf16[8,256,256]{2,1,0:T(8,128)(2,1)}, bf16[8,256,256]{2,1,0:T(8,128)(2,1)S(1)}, u32[]{:S(2)}) copy-start(bf16[8,256,256]{2,1,0:T(8,128)(2,1)S(1)} %get-tuple-element.22.vlo_ref) | copy-start | bytes 3145732
  26.2 0.8 %copy-start.6 = (bf16[512,512]{1,0:T(8,128)(2,1)}, bf16[512,512]{1,0:T(8,128)(2,1)S(1)}, u32[]{:S(2)}) copy-start(bf16[512,512]{1,0:T(8,128)(2,1)S(1)} %get-tuple-element.15.lhi_ref) | copy-start | bytes 1572868
  27.0 0.8 %copy-start.8 = (bf16[512,512]{1,0:T(8,128)(2,1)}, bf16[512,512]{1,0:T(8,128)(2,1)S(1)}, u32[]{:S(2)}) copy-start(bf16[512,512]{1,0:T(8,128)(2,1)S(1)} %get-tuple-element.16.llo_ref) | copy-start | bytes 1572868
  27.8 0.8 %copy-start.10 = (bf16[512,512]{1,0:T(8,128)(2,1)}, bf16[512,512]{1,0:T(8,128)(2,1)S(1)}, u32[]{:S(2)}) copy-start(bf16[512,512]{1,0:T(8,128)(2,1)S(1)} %get-tuple-element.17.ihi_ref) | copy-start | bytes 1572868
  28.6 0.8 %copy-start.12 = (bf16[512,512]{1,0:T(8,128)(2,1)}, bf16[512,512]{1,0:T(8,128)(2,1)S(1)}, u32[]{:S(2)}) copy-start(bf16[512,512]{1,0:T(8,128)(2,1)S(1)} %get-tuple-element.18.ilo_ref) | copy-start | bytes 1572868
  29.4 0.6 copy-start.19
  30.0 1.2 %copy-start.1 = (bf16[8,256,256]{2,1,0:T(8,128)(2,1)S(1)}, bf16[8,256,256]{2,1,0:T(8,128)(2,1)}, u32[]{:S(2)}) copy-start(bf16[8,256,256]{2,1,0:T(8,128)(2,1)} %copy-done) | copy-start | bytes 3145732
  31.3 1.2 %copy-start.3 = (bf16[8,256,256]{2,1,0:T(8,128)(2,1)S(1)}, bf16[8,256,256]{2,1,0:T(8,128)(2,1)}, u32[]{:S(2)}) copy-start(bf16[8,256,256]{2,1,0:T(8,128)(2,1)} %copy-done.2) | copy-start | bytes 3145732
  32.5 1.0 %copy-start.7 = (bf16[512,512]{1,0:T(8,128)(2,1)S(1)}, bf16[512,512]{1,0:T(8,128)(2,1)}, u32[]{:S(2)}) copy-start(bf16[512,512]{1,0:T(8,128)(2,1)} %copy-done.6) | copy-start | bytes 1572868
  33.5 1.0 %copy-start.9 = (bf16[512,512]{1,0:T(8,128)(2,1)S(1)}, bf16[512,512]{1,0:T(8,128)(2,1)}, u32[]{:S(2)}) copy-start(bf16[512,512]{1,0:T(8,128)(2,1)} %copy-done.8) | copy-start | bytes 1572868
  34.6 1.0 %copy-start.11 = (bf16[512,512]{1,0:T(8,128)(2,1)S(1)}, bf16[512,512]{1,0:T(8,128)(2,1)}, u32[]{:S(2)}) copy-start(bf16[512,512]{1,0:T(8,128)(2,1)} %copy-done.10) | copy-start | bytes 1572868
  35.6 1.0 %copy-start.13 = (bf16[512,512]{1,0:T(8,128)(2,1)S(1)}, bf16[512,512]{1,0:T(8,128)(2,1)}, u32[]{:S(2)}) copy-start(bf16[512,512]{1,0:T(8,128)(2,1)} %copy-done.12) | copy-start | bytes 1572868
  36.6 0.8 %copy-start.20 = (f32[64,128]{1,0:T(8,128)S(1)}, f32[64,128]{1,0:T(8,128)}, u32[]{:S(2)}) copy-start(f32[64,128]{1,0:T(8,128)} %copy-done.19) | copy-start | bytes 98308
where the time goes:
time: 63.7 us; the launch traced here: 62.8 us
  blocking collectives  19.1 us (30%)
  local copies, waits for them, and re-layouts  18.3 us (29%)
  Pallas kernels  11.5 us (18%)
  starting transfers between devices  10.8 us (17%)
  waiting for transfers between devices  1.4 us (2%)
  other arithmetic  0.97 us (2%)
  between operations  0.74 us (1%)
    all_to_all x1, blocking collectives, local(): back = lax.all_to_all(done, VEL, split_axis=0, concat_axis=0, tiled=True)  19.1 us
    unnamed x48, local copies, waits for them, and re-layouts  18.3 us
    all_to_all x1, starting transfers between devices, local(): cells = lax.all_to_all(mine, VEL, split_axis=0, concat_axis=0, tiled=True)  8.89 us
    pallas_call x1, Pallas kernels, collide(): pl.pallas_call(collide_kernel, out_shape=shape(16, 64, 128), in_specs=[VM...  5.39 us
    pallas_call x1, Pallas kernels, make_tables(): pl.pallas_call(tables_kernel, out_shape=[half] * 4 + [eight] * 4 + [shape...  3.5 us
    ppermute x1, starting transfers between devices, local(): halo = lax.ppermute(edge, ('space',) + VEL, pairs)  1.92 us
    pallas_call x1, Pallas kernels, transport(): pl.pallas_call(transport_kernel, out_shape=shape(16, 64, 128), in_specs=[...  1.66 us
    ppermute x1, waiting for transfers between devices, local(): halo = lax.ppermute(edge, ('space',) + VEL, pairs)  1.4 us
  transfers between devices with their start and end apart: 2, of which 1 were waited for; matrix products, arithmetic and copies ran while one was open for 0% of the time, Pallas kernels for 6%

commit v1 on v0

v1 whole, which is shorter than its diff:
```python
import math

import jax
import jax.numpy as jnp
import numpy as np
from jax import lax
from jax.experimental import pallas as pl
from jax.experimental.pallas import tpu as pltpu
from jax.sharding import Mesh
from jax.sharding import PartitionSpec as P

NV = 32
BLOCK_CELLS = 16
KERN = 5
VEL = ("vel_0", "vel_1")
COURANT_MAX = 0.95
STEP_SCALE = 0.25
F32 = jnp.float32
BF16 = jnp.bfloat16
SLOT = 64


def constant_rows():
    lane = np.arange(128)
    y4, z = lane // 32, lane % 32
    base = ((8 * np.outer(y4, y4) + np.outer(z, z)) % 32) * (2.0 * math.pi / 32)
    row = np.arange(32)
    x = 2 * (row % 16) + row // 16
    left = (np.outer(np.arange(32), x) % 32) * (2.0 * math.pi / 32)
    c, s = np.cos(left), np.sin(left)
    forward = np.block([[c, s], [-s, c]])
    neg = (32 - z) % 32
    flips = []
    for other in ((4 - y4) % 4, 3 - y4):
        flip = np.zeros((128, 128))
        flip[other * 32 + neg, lane] = 1.0
        flips.append(flip)
    both = np.concatenate([forward, forward.T], axis=1)
    return np.concatenate([np.cos(base), np.sin(base), both] + flips, axis=0).astype(np.float32)


def split(a):
    hi = a.astype(BF16)
    lo = (a - hi.astype(F32)).astype(BF16)
    return hi, lo


def dot(a, b):
    return jnp.dot(a, b, preferred_element_type=F32)


def upwind(f0, f1, f2, a):
    once = f0 - a * (f0 - f1)
    beside = f1 - a * (f1 - f2)
    return once - a * (once - beside)


def transport_kernel(side_ref, courant_ref, dist_ref, out_ref, edge_ref, raw):
    step = side_ref[0]
    zero = jnp.zeros((32, 128), F32)
    raw[0:32, :] = zero
    raw[66 * 16 : 68 * 16, :] = zero
    for tile in range(8):
        for j in range(16):
            raw[pl.ds((8 * tile + 2) * 16 + j, 8, stride=16), :] = dist_ref[
                8 * tile : 8 * tile + 8, 128 * j : 128 * j + 128
            ]
    for cell in range(64):
        for half in range(2):
            here = (cell + 2) * 16 + 8 * half
            f0 = raw[pl.ds(here, 8), :]
            f1 = raw[pl.ds(pl.multiple_of(here + 16 * step, 8), 8), :]
            f2 = raw[pl.ds(pl.multiple_of(here + 32 * step, 8), 8), :]
            out_ref[cell // 4, pl.ds(2 * (cell % 4) + half, 8, stride=8), :] = upwind(
                f0, f1, f2, courant_ref[half]
            )
    first = pl.multiple_of(jnp.where(step < 0, 32, 62 * 16), 16)
    edge_ref[...] = raw[pl.ds(first, SLOT), :]


def edge_kernel(side_ref, courant_ref, edge_ref, halo_ref, _, out_ref, raw, slot, sem):
    step = side_ref[0]
    raw[32:96, :] = edge_ref[...]
    at = pl.multiple_of(jnp.where(step < 0, 0, 96), 16)
    for j in range(16):
        raw[pl.ds(at + j, 2, stride=16), :] = halo_ref[:, 128 * j : 128 * j + 128]
    for cell in range(4):
        for half in range(2):
            here = (cell + 2) * 16 + 8 * half
            f0 = raw[pl.ds(here, 8), :]
            f1 = raw[pl.ds(pl.multiple_of(here + 16 * step, 8), 8), :]
            f2 = raw[pl.ds(pl.multiple_of(here + 32 * step, 8), 8), :]
            slot[pl.ds(2 * cell + half, 8, stride=8), :] = upwind(f0, f1, f2, courant_ref[half])
    copy = pltpu.make_async_copy(slot, out_ref.at[jnp.where(step < 0, 0, 15)], sem)
    copy.start()
    copy.wait()


def tables_kernel(
    where_ref, order_ref, kern_ref, const_ref, v_ref, left_ref, ks_ref, mask_ref, rows, turned
):
    position = lax.broadcasted_iota(jnp.int32, (1, 64), 1)
    first = position < BLOCK_CELLS * where_ref[1]
    for c in range(4):
        hit = jnp.where(first & (order_ref[...] == 4 * where_ref[0] + c), STEP_SCALE, 0.0)
        mask_ref[8 * c : 8 * c + 8, :] = jnp.broadcast_to(jnp.sum(hit, axis=1, keepdims=True), (8, 128))
    c0, s0 = const_ref[0:128, :], const_ref[128:256, :]
    lane_y4 = lax.broadcasted_iota(jnp.int32, (1, 128), 1) // 32
    for k8 in range(8):
        cvec, svec = turn(k8, lane_y4)
        for i, (cc, ss) in enumerate(
            zip(split(cvec * c0 - svec * s0), split(cvec * s0 + svec * c0))
        ):
            v_ref[k8, i, 0] = cc
            v_ref[k8, i, 1] = ss
    lhi, llo = split(const_ref[256:320, :])
    for i in range(2):
        part = slice(64 * i, 64 * i + 64)
        left_ref[i] = jnp.concatenate([lhi[:, part], lhi[:, part], llo[:, part]], axis=1)
    for kx in range(32):
        for ch in range(8):
            at = kx * 8 + ch
            back = ((32 - kx) % 32) * 8 + ch
            tile = kern_ref[:, at * 128 : at * 128 + 128]
            rows[pl.ds(at, KERN, stride=256), :] = tile
            turned[pl.ds(back, KERN, stride=256), :] = tile
    group = lax.broadcasted_iota(jnp.int32, (32, 128), 1) // 32

    def ordered(src, t, k8):
        g, h = k8 % 4, k8 // 4
        out = None
        for k4 in range(4):
            piece = src[pl.ds(t * 256 + 2 * k4 + h, 32, stride=8), :]
            if k4 != g:
                piece = pltpu.roll(piece, ((k4 - g) % 4) * 32, 1)
            out = piece if out is None else jnp.where(group == k4, piece, out)
        return out

    scale = 0.5 / NV**3
    for k8 in range(8):
        at = 320 if k8 == 0 else 448
        flip = const_ref[at : at + 128, :].astype(BF16)
        for t in range(KERN):
            straight = ordered(rows, t, k8)
            other = ordered(turned, t, (8 - k8) % 8)
            hi, lo = split(other)
            ks_ref[k8, t] = scale * (straight + (dot(hi, flip) + dot(lo, flip)))


def turn(k8, lane_y4):
    cvec = jnp.full((1, 128), 1.0, F32)
    svec = jnp.full((1, 128), 0.0, F32)
    for y4 in range(1, 4):
        angle = 2 * math.pi * y4 * k8 / 32
        cvec = jnp.where(lane_y4 == y4, math.cos(angle), cvec)
        svec = jnp.where(lane_y4 == y4, math.sin(angle), svec)
    return cvec, svec


def fft8(re, im):
    h = math.sqrt(0.5)
    ar = [re[j] + re[j + 4] for j in range(4)]
    ai = [im[j] + im[j + 4] for j in range(4)]
    dr = [re[j] - re[j + 4] for j in range(4)]
    di = [im[j] - im[j + 4] for j in range(4)]
    br = [dr[0], h * (dr[1] + di[1]), di[2], h * (di[3] - dr[3])]
    bi = [di[0], h * (di[1] - dr[1]), -dr[2], -h * (di[3] + dr[3])]
    outr, outi = [None] * 8, [None] * 8
    for odd, cr, ci in ((0, ar, ai), (1, br, bi)):
        s0r, s0i = cr[0] + cr[2], ci[0] + ci[2]
        s1r, s1i = cr[0] - cr[2], ci[0] - ci[2]
        s2r, s2i = cr[1] + cr[3], ci[1] + ci[3]
        s3r, s3i = ci[1] - ci[3], cr[3] - cr[1]
        outr[odd], outi[odd] = s0r + s2r, s0i + s2i
        outr[4 + odd], outi[4 + odd] = s0r - s2r, s0i - s2i
        outr[2 + odd], outi[2 + odd] = s1r + s3r, s1i + s3i
        outr[6 + odd], outi[6 + odd] = s1r - s3r, s1i - s3i
    return outr, outi


def right(v_ref, k8, i, inverse):
    c, s = v_ref[k8, i, 0], v_ref[k8, i, 1]
    up, down = (s, -s) if inverse else (-s, s)
    return jnp.concatenate(
        [jnp.concatenate([c, up], axis=1), jnp.concatenate([down, c], axis=1)], axis=0
    )


def collide_kernel(x_ref, v_ref, left_ref, ks_ref, mask_ref, out_ref, fwd, mid, back):
    for p in range(2):
        lanes = slice(128 * p, 128 * p + 128)
        for x2 in range(2):
            def cell_rows(ch, cell):
                at = 8 * ch + 2 * (2 * p + cell) + x2
                return x_ref[pl.ds(at, 16, stride=SLOT), :]

            re, im = fft8([cell_rows(ch, 0) for ch in range(8)], [cell_rows(ch, 1) for ch in range(8)])
            for k8 in range(8):
                for ri, val in ((0, re[k8]), (1, im[k8])):
                    hi, lo = split(val)
                    at = 32 * ri + 16 * x2
                    fwd[k8, at : at + 16, lanes] = hi
                    fwd[k8, 64 + at : 80 + at, lanes] = lo
                    fwd[k8, 128 + at : 144 + at, lanes] = hi
    lane_y4 = lax.broadcasted_iota(jnp.int32, (1, 128), 1) // 32
    whi, wlo = right(v_ref, 0, 0, False), right(v_ref, 0, 1, False)
    for k8 in range(8):
        y = dot(left_ref[0], fwd[k8])
        cvec, svec = turn(k8, lane_y4)
        fields = []
        for p in range(2):
            re, im = y[0:32, 128 * p : 128 * p + 128], y[32:64, 128 * p : 128 * p + 128]
            if k8:
                re, im = re * cvec + im * svec, im * cvec - re * svec
            fields.append(jnp.concatenate([re, im], axis=1))
        fhi, flo = split(jnp.concatenate(fields, axis=0))
        spectrum = dot(fhi, whi) + dot(flo, whi) + dot(fhi, wlo)
        parts = []
        for t in range(KERN):
            ks = ks_ref[k8, t]
            ks = jnp.concatenate([ks, ks], axis=1)
            parts += [spectrum[0:32] * ks, spectrum[32:64] * ks]
        ghi, glo = split(jnp.concatenate(parts, axis=0))
        vhi, vlo = right(v_ref, k8, 0, True), right(v_ref, k8, 1, True)
        hi, lo = split(dot(ghi, vhi) + dot(glo, vhi) + dot(ghi, vlo))
        for n in range(2 * KERN):
            lanes = slice(128 * n, 128 * n + 128)
            for ri in range(2):
                val = hi[32 * n : 32 * n + 32, 128 * ri : 128 * ri + 128]
                mid[32 * ri : 32 * ri + 32, lanes] = val
                mid[128 + 32 * ri : 160 + 32 * ri, lanes] = val
                mid[64 + 32 * ri : 96 + 32 * ri, lanes] = lo[
                    32 * n : 32 * n + 32, 128 * ri : 128 * ri + 128
                ]
        back[k8] = dot(left_ref[1], mid[...])
    for p in range(2):
        for x2 in range(2):
            for vh in range(2):
                def part(t):
                    lanes = slice(256 * t + 128 * p, 256 * t + 128 * p + 128)
                    at = 16 * x2 + 8 * vh
                    re = [back[k8, at : at + 8, lanes] for k8 in range(8)]
                    im = [back[k8, 32 + at : 40 + at, lanes] for k8 in range(8)]
                    im, re = fft8(im, re)
                    return re + im

                total = [a * b for a, b in zip(part(0), part(1))]
                second = part(2)
                total = [a + b * c for a, b, c in zip(total, second, part(3))]
                loss = part(4)
                for cell in range(2):
                    mask = mask_ref[8 * (2 * p + cell) : 8 * (2 * p + cell) + 8, :]
                    for ch in range(8):
                        at = vh * 8 * SLOT + 8 * ch + 2 * (2 * p + cell) + x2
                        f = x_ref[pl.ds(at, 8, stride=SLOT), :]
                        i = 8 * cell + ch
                        out_ref[pl.ds(at, 8, stride=SLOT), :] = f + mask * (total[i] - f * loss[i])


def place_kernel(in_ref, out_ref):
    for tile in range(8):
        for x2 in range(2):
            for ch in range(8):
                j = 8 * x2 + ch
                for k in range(2):
                    at = (2 * tile + k) * SLOT + 8 * ch + x2
                    out_ref[8 * tile + 4 * k : 8 * tile + 4 * k + 4, 128 * j : 128 * j + 128] = in_ref[
                        pl.ds(at, 4, stride=2), :
                    ]


VM = pl.BlockSpec(memory_space=pltpu.VMEM)
SM = pl.BlockSpec(memory_space=pltpu.SMEM)
ANY = pl.BlockSpec(memory_space=pl.ANY)


def shape(*dims, dtype=F32):
    return jax.ShapeDtypeStruct(dims, dtype)


def params(mib):
    return pltpu.CompilerParams(vmem_limit_bytes=mib << 20)


def transport(side, courant, dist):
    return pl.pallas_call(
        transport_kernel,
        out_shape=[shape(16, SLOT, 128), shape(SLOT, 128)],
        in_specs=[SM, SM, VM],
        out_specs=[VM, VM],
        scratch_shapes=[pltpu.VMEM((68 * 16, 128), F32)],
        compiler_params=params(8),
        cost_estimate=pl.CostEstimate(flops=4000000, bytes_accessed=1 << 20, transcendentals=0),
        name="transport",
    )(side, courant, dist)


def edges(side, courant, edge, halo, mine):
    return pl.pallas_call(
        edge_kernel,
        out_shape=shape(16, SLOT, 128),
        in_specs=[SM, SM, VM, VM, ANY],
        out_specs=ANY,
        input_output_aliases={4: 0},
        scratch_shapes=[
            pltpu.VMEM((128, 128), F32),
            pltpu.VMEM((SLOT, 128), F32),
            pltpu.SemaphoreType.DMA,
        ],
        compiler_params=params(8),
        name="edges",
    )(side, courant, edge, halo, mine)


def make_tables(where, order, kernels):
    return pl.pallas_call(
        tables_kernel,
        out_shape=[
            shape(8, 2, 2, 128, 128, dtype=BF16),
            shape(2, 64, 192, dtype=BF16),
            shape(8, KERN, 32, 128),
            shape(32, 128),
        ],
        in_specs=[SM] + [VM] * 3,
        out_specs=[VM] * 4,
        scratch_shapes=[pltpu.VMEM((KERN * 256, 128), F32), pltpu.VMEM((KERN * 256, 128), F32)],
        compiler_params=params(12),
        cost_estimate=pl.CostEstimate(flops=8000000, bytes_accessed=4 << 20, transcendentals=0),
        name="tables",
    )(where, order, kernels, jnp.asarray(constant_rows()))


def collide(x, tables):
    return pl.pallas_call(
        collide_kernel,
        out_shape=shape(16 * SLOT, 128),
        in_specs=[VM] * 5,
        out_specs=VM,
        scratch_shapes=[
            pltpu.VMEM((8, 192, 256), BF16),
            pltpu.VMEM((192, 1280), BF16),
            pltpu.VMEM((8, 64, 1280), F32),
        ],
        compiler_params=params(16),
        name="collide",
    )(x.reshape(16 * SLOT, 128), *tables).reshape(16, SLOT, 128)


def place(x):
    return pl.pallas_call(
        place_kernel,
        out_shape=shape(64, 2048),
        in_specs=[VM],
        out_specs=VM,
        compiler_params=params(8),
        name="place",
    )(x.reshape(16 * SLOT, 128))


def local(distribution, collision_order, collision_blocks, kernels):
    v = lax.axis_index(VEL)
    rising = v >= 8
    x = 2 * v + lax.iota(jnp.int32, 2)
    courant = jnp.abs(COURANT_MAX * (2.0 * x.astype(F32) - (NV - 1)) / (NV - 1))
    side = jnp.where(rising, -1, 1).astype(jnp.int32)[None]
    edge_rows = jnp.where(rising, distribution[62:64], distribution[0:2])
    pairs = []
    for s in range(16):
        for u in range(16):
            to = s + 1 if u >= 8 else s - 1
            if 0 <= to < 16:
                pairs.append((s * 16 + u, to * 16 + u))
    halo = lax.ppermute(edge_rows, ("space",) + VEL, pairs)
    mine, edge = transport(side, courant, distribution)
    mine = edges(side, courant, edge, halo, mine)
    where = jnp.stack([v.astype(jnp.int32), collision_blocks[0]])
    tables = make_tables(where, collision_order, kernels)
    cells = lax.all_to_all(mine, VEL, split_axis=0, concat_axis=0, tiled=True)
    done = collide(cells, tables)
    back = lax.all_to_all(done, VEL, split_axis=0, concat_axis=0, tiled=True)
    return place(back)


def solution(mesh):
    finer = Mesh(mesh.devices.reshape(mesh.shape["space"], 4, 4), ("space", "vel_0", "vel_1"))
    in_specs = (P("space", VEL), P("space", None), P("space"), P())
    out_specs = P("space", VEL)
    return jax.shard_map(local, mesh=finer, in_specs=in_specs, out_specs=out_specs, check_vma=False)
```

time: 63.7 us -> 50.9 us (0.80)
  local copies, waits for them, and re-layouts: 18.3 us -> 2.57 us
  waiting for transfers between devices: 1.4 us -> 6.53 us
  blocking collectives: 19.1 us -> 16.2 us
  Pallas kernels: 11.5 us -> 14 us
  starting transfers between devices: 10.8 us -> 9.36 us
    unnamed x48 -> x8, local copies, waits for them, and re-layouts: 18.3 us -> 2.57 us
    all_to_all x1, waiting for transfers between devices: 0.01 us -> 6.52 us  [local(): cells = lax.all_to_all(mine, VEL, split_axis=0, concat_axis=0, tiled=True)]
    all_to_all x1, blocking collectives: 19.1 us -> 16.2 us  [local(): back = lax.all_to_all(done, VEL, split_axis=0, concat_axis=0, tiled=True)]
    pallas_call x3 -> x4, Pallas kernels: 10.6 us -> 13.1 us  [the longest x1 7.63 us: collide(): pl.pallas_call(collide_kernel, out_shape=shape(16 * SLOT, 128), in_specs=...]
    all_to_all x1, starting transfers between devices: 8.89 us -> 7.44 us  [local(): cells = lax.all_to_all(mine, VEL, split_axis=0, concat_axis=0, tiled=True)]
    ppermute x1, waiting for transfers between devices: 1.4 us -> 0.01 us  [local(): halo = lax.ppermute(edge_rows, ('space',) + VEL, pairs)]
  transfers between devices with their start and end apart: 2 -> 2, of which waited for: 1 -> 1; matrix products, arithmetic and copies ran while one was open for 0% -> 0% of each run, Pallas kernels for 6% -> 9%
where the time goes in v1:
time: 50.9 us; the launch traced here: 50.4 us
  blocking collectives  16.2 us (32%)
  Pallas kernels  14 us (28%)
  starting transfers between devices  9.36 us (18%)
  waiting for transfers between devices  6.53 us (13%)
  local copies, waits for them, and re-layouts  2.57 us (5%)
  other arithmetic  0.97 us (2%)
  between operations  0.73 us (1%)
    all_to_all x1, blocking collectives, local(): back = lax.all_to_all(done, VEL, split_axis=0, concat_axis=0, tiled=True)  16.2 us
    pallas_call x1, Pallas kernels, collide(): pl.pallas_call(collide_kernel, out_shape=shape(16 * SLOT, 128), in_specs=...  7.63 us
    all_to_all x1, starting transfers between devices, local(): cells = lax.all_to_all(mine, VEL, split_axis=0, concat_axis=0, tiled=True)  7.44 us
    all_to_all x1, waiting for transfers between devices, local(): cells = lax.all_to_all(mine, VEL, split_axis=0, concat_axis=0, tiled=True)  6.52 us
    pallas_call x1, Pallas kernels, make_tables(): pl.pallas_call(tables_kernel, out_shape=[shape(8, 2, 2, 128, 128, dtype=B...  2.63 us
    unnamed x8, local copies, waits for them, and re-layouts  2.57 us
    ppermute x1, starting transfers between devices, local(): halo = lax.ppermute(edge_rows, ('space',) + VEL, pairs)  1.92 us
    pallas_call x1, Pallas kernels, transport(): pl.pallas_call(transport_kernel, out_shape=[shape(16, SLOT, 128), shape(S...  1.67 us
  transfers between devices with their start and end apart: 2, of which 1 were waited for; matrix products, arithmetic and copies ran while one was open for 0% of the time, Pallas kernels for 9%

profile of v1, /device:TPU:96, one launch (start us, length us, event | category | flops | bytes accessed | tf_op | source)
XLA Modules:
  0.0 50.4 jit_solution(8177911949667021518)
XLA Ops:
  0.0 0.9 %slice_select_fusion = f32[2,2048]{1,0:T(2,128)S(1)} fusion(f32[64,2048]{1,0:T(8,128)} %dist_ref.1, pred[]{:T(512)S(6)} %ge.3), kind=kLoop, calls=%fused_computation | loop fusion | flops 4096 | bytes 49153 | tf_op jit(solution)/shard_map/jit(_where)/select_n | solution.py:366
  0.9 1.9 %collective-permute-start = (f32[2,2048]{1,0:T(2,128)S(1)}, f32[2,2048]{1,0:T(2,128)S(1)}, u32[]{:S(2)}, u32[]{:S(2)}) collective-permute-start(f32[2,2048]{1,0:T(2,128)S(1)} %slice_select_fusion), channel_id=1, source_target_pairs={{8,24},{9,25},{10,26},{11,27},{12,28},{13,29},{14,30},{15,31},{16,... | collective-permute-start | bytes 49160 | tf_op jit(solution)/shard_map/ppermute | solution.py:373
  2.8 0.0 copy-start.1
  2.8 1.0 %copy-done.1 = f32[64,2048]{1,0:T(8,128)S(1)} copy-done((f32[64,2048]{1,0:T(8,128)S(1)}, f32[64,2048]{1,0:T(8,128)}, u32[]{:S(2)}) %copy-start.1) | copy-done | bytes 524312
  3.9 1.7 %transport.1 = (f32[16,64,128]{2,1,0:T(8,128)}, f32[64,128]{1,0:T(8,128)S(1)}) custom-call(s32[1]{0:T(128)} %bitcast.side_ref, f32[2]{0:T(128)S(1)} %multiply_abs_fusion.courant_ref, f32[64,2048]{1,0:T(8,128)S(1)} %copy-done.1), custom_call_target="tpu_custom_call" | custom-call | flops 4000000 | bytes 1048576 | tf_op jit(solution)/shard_map/transport/pallas_call | solution.py:286
  5.5 0.0 collective-permute-done.halo_ref
  5.6 0.0 copy-start
  5.6 1.2 %edges.1 = f32[16,64,128]{2,1,0:T(8,128)} custom-call(s32[1]{0:T(128)} %bitcast.side_ref, f32[2]{0:T(128)S(1)} %multiply_abs_fusion.courant_ref, f32[64,128]{1,0:T(8,128)S(1)} %get-tuple-element.11.edge_ref, f32[2,2048]{1,0:T(2,128)S(1)} %collective-permute-done.halo_ref, f32[16,64,128]{2,1,0:T(8,128)} %get-tuple-element.12._), custom_call_target="tpu_custom_call", output_to_operand_aliasing={{}: (4, {})} | custom-call | tf_op jit(solution)/shard_map/edges/pallas_call | solution.py:299
  6.8 7.4 %all-to-all-start = ((f32[16,64,128]{2,1,0:T(8,128)}), f32[16,64,128]{2,1,0:T(8,128)S(1)}, u32[]{:S(2)}, u32[]{:S(2)}) async-start(f32[16,64,128]{2,1,0:T(8,128)} %edges.1), calls=%async_computation | async-start | bytes 1048576 | tf_op jit(solution)/shard_map/all_to_all | solution.py:378
  14.8 0.0 copy-start.3
  14.9 0.1 pad_add_fusion.where_ref
  14.9 0.0 copy-done
  14.9 0.6 %copy-done.3 = s32[1,64]{1,0:T(1,128)S(1)} copy-done((s32[1,64]{1,0:T(1,128)S(1)}, s32[1,64]{1,0:T(1,128)}, u32[]{:S(2)}) %copy-start.3) | copy-done | bytes 280
  15.5 0.0 copy-start.2
  15.5 1.0 %copy-done.2 = f32[576,128]{1,0:T(8,128)S(1)} copy-done((f32[576,128]{1,0:T(8,128)S(1)}, f32[576,128]{1,0:T(8,128)}, u32[]{:S(2)}) %copy-start.2) | copy-done | bytes 294936
  16.5 2.6 %tables.1 = (bf16[8,2,2,128,128]{4,3,2,1,0:T(8,128)(2,1)S(1)}, bf16[2,64,192]{2,1,0:T(8,128)(2,1)S(1)}, f32[8,5,32,128]{3,2,1,0:T(8,128)S(1)}, f32[32,128]{1,0:T(8,128)S(1)}) custom-call(s32[2]{0:T(128)S(1)} %pad_add_fusion.where_ref, s32[1,64]{1,0:T(1,128)S(1)} %copy-done.3, f32[5,32768]{1,0:T(8,128)S(1)} %copy-done, f32[576,128]{1,0:T(8,128)S(1)} %copy-done.2), custom_call_target="tpu_custom_call" | custom-call | flops 8000000 | bytes 4194304 | tf_op jit(solution)/shard_map/tables/pallas_call | solution.py:316
  19.1 6.5 %all-to-all-done = f32[16,64,128]{2,1,0:T(8,128)S(1)} async-done(((f32[16,64,128]{2,1,0:T(8,128)}), f32[16,64,128]{2,1,0:T(8,128)S(1)}, u32[]{:S(2)}, u32[]{:S(2)}) %all-to-all-start) | async-done | bytes 524320 | tf_op jit(solution)/shard_map/all_to_all | solution.py:378
  25.6 7.6 %collide.1 = f32[1024,128]{1,0:T(8,128)S(1)} custom-call(f32[1024,128]{1,0:T(8,128)S(1)} %bitcast.6, bf16[8,2,2,128,128]{4,3,2,1,0:T(8,128)(2,1)S(1)} %get-tuple-element.13.v_ref, bf16[2,64,192]{2,1,0:T(8,128)(2,1)S(1)} %get-tuple-element.14.left_ref, f32[8,5,32,128]{3,2,1,0:T(8,128)S(1)} %get-tuple-element.15.ks_ref, f32[32,128]{1,0:T(8,128)S(1)} %get-tuple-element.16.mask_ref), custom_call_target="tpu_custom_call" | custom-call | tf_op jit(solution)/shard_map/collide/pallas_call | solution.py:334
  33.3 16.2 %all_to_all.10 = f32[16,64,128]{2,1,0:T(8,128)S(1)} all-to-all(f32[16,64,128]{2,1,0:T(8,128)S(1)} %bitcast.7), channel_id=1, replica_groups=mesh['space'=16,'vel_0'=4,'vel_1'=4] {'vel_0','vel_1'}, dimensions={0} | all-to-all | bytes 1048576 | tf_op jit(solution)/shard_map/all_to_all | solution.py:380
  49.5 0.9 %place.1 = f32[64,2048]{1,0:T(8,128)} custom-call(f32[1024,128]{1,0:T(8,128)S(1)} %bitcast.5), custom_call_target="tpu_custom_call" | custom-call | tf_op jit(solution)/shard_map/place/pallas_call | solution.py:350
  (1 shorter events, 0.0 us)
Async XLA Ops:
  0.9 4.7 %collective-permute-start = (f32[2,2048]{1,0:T(2,128)S(1)}, f32[2,2048]{1,0:T(2,128)S(1)}, u32[]{:S(2)}, u32[]{:S(2)}) collective-permute-start(f32[2,2048]{1,0:T(2,128)S(1)} %slice_select_fusion), channel_id=1, source_target_pairs={{8,24},{9,25},{10,26},{11,27},{12,28},{13,29},{14,30},{15,31},{16,... | collective-permute-start | bytes 49160 | tf_op jit(solution)/shard_map/ppermute | solution.py:373
  2.8 1.0 %copy-start.1 = (f32[64,2048]{1,0:T(8,128)S(1)}, f32[64,2048]{1,0:T(8,128)}, u32[]{:S(2)}) copy-start(f32[64,2048]{1,0:T(8,128)} %dist_ref.1) | copy-start | bytes 1572868
  5.6 9.4 %copy-start = (f32[5,32768]{1,0:T(8,128)S(1)}, f32[5,32768]{1,0:T(8,128)}, u32[]{:S(2)}) copy-start(f32[5,32768]{1,0:T(8,128)} %kern_ref.1) | copy-start | bytes 1966084
  6.8 18.9 %all-to-all-start = ((f32[16,64,128]{2,1,0:T(8,128)}), f32[16,64,128]{2,1,0:T(8,128)S(1)}, u32[]{:S(2)}, u32[]{:S(2)}) async-start(f32[16,64,128]{2,1,0:T(8,128)} %edges.1), calls=%async_computation | async-start | bytes 1048576 | tf_op jit(solution)/shard_map/all_to_all | solution.py:378
  14.8 0.7 %copy-start.3 = (s32[1,64]{1,0:T(1,128)S(1)}, s32[1,64]{1,0:T(1,128)}, u32[]{:S(2)}) copy-start(s32[1,64]{1,0:T(1,128)} %order_ref.1) | copy-start | bytes 772
  15.5 1.0 %copy-start.2 = (f32[576,128]{1,0:T(8,128)S(1)}, f32[576,128]{1,0:T(8,128)}, u32[]{:S(2)}) copy-start(f32[576,128]{1,0:T(8,128)} %constant.28.clone.const_ref) | copy-start | bytes 884740

commit v2 on v1

v2 whole, which is shorter than its diff:
```python
import math

import jax
import jax.numpy as jnp
import numpy as np
from jax import lax
from jax.experimental import pallas as pl
from jax.experimental.pallas import tpu as pltpu
from jax.sharding import PartitionSpec as P

NV = 32
BLOCK_CELLS = 16
KERN = 5
COURANT_MAX = 0.95
STEP_SCALE = 0.25
F32 = jnp.float32
BF16 = jnp.bfloat16
SLOT = 64

THERE = (15, 14, 13, 12, 11, 10, 9, 8, 7, 6, 5, 4, 3, 2, 1, 0)
BACK = (15, 14, 13, 12, 11, 10, 9, 8, 7, 6, 5, 4, 3, 2, 1, 0)
THERE_AT = [THERE.index(v) for v in range(16)]
BACK_AT = [BACK.index(v) for v in range(16)]


def constant_rows():
    lane = np.arange(128)
    y4, z = lane // 32, lane % 32
    x = 2 * (lane // 8) + lane % 2
    unit = 2.0 * math.pi / 32
    parts = []
    for phase in (8 * np.outer(y4, y4) + np.outer(z, z), np.outer(np.arange(32), x), np.outer(x, z)):
        parts += [np.cos((phase % 32) * unit), np.sin((phase % 32) * unit)]
    neg = (32 - z) % 32
    for other in ((4 - y4) % 4, 3 - y4):
        flip = np.zeros((128, 128))
        flip[other * 32 + neg, lane] = 1.0
        parts.append(flip)
    return np.concatenate(parts, axis=0).astype(np.float32)


def split(a):
    hi = a.astype(BF16)
    lo = (a - hi.astype(F32)).astype(BF16)
    return hi, lo


def dot(a, b):
    return jnp.dot(a, b, preferred_element_type=F32)


def dot3(ahi, alo, bhi, blo):
    return dot(ahi, bhi) + dot(ahi, blo) + dot(alo, bhi)


def upwind(f0, f1, f2, a):
    once = f0 - a * (f0 - f1)
    beside = f1 - a * (f1 - f2)
    return once - a * (once - beside)


def sweeps(raw, cells, first, step, courant_ref, store):
    for cell in range(cells):
        for half in range(2):
            here = first + cell * 16 + 8 * half
            f0 = raw[pl.ds(here, 8), :]
            f1 = raw[pl.ds(pl.multiple_of(here + 16 * step, 8), 8), :]
            f2 = raw[pl.ds(pl.multiple_of(here + 32 * step, 8), 8), :]
            store(cell, half, upwind(f0, f1, f2, courant_ref[half]))


def transport_kernel(
    side_ref, courant_ref, dist_ref, out_ref, edge_ref, raw, slots, out_sem
):
    step = side_ref[0]
    zero = jnp.zeros((32, 128), F32)
    raw[0:32, :] = zero
    raw[66 * 16 : 68 * 16, :] = zero
    for tile in range(8):
        for j in range(16):
            raw[pl.ds((8 * tile + 2) * 16 + j, 8, stride=16), :] = dist_ref[
                8 * tile : 8 * tile + 8, 128 * j : 128 * j + 128
            ]
    stores = [
        pltpu.make_async_copy(slots.at[i], out_ref.at[i], out_sem.at[i]) for i in range(16)
    ]

    def store(cell, half, value):
        slots[THERE_AT[cell // 4], pl.ds(2 * (cell % 4) + half, 8, stride=8), :] = value
        if cell % 4 == 3 and half == 1:
            stores[THERE_AT[cell // 4]].start()

    sweeps(raw, 64, 32, step, courant_ref, store)
    edge_ref[...] = raw[pl.ds(pl.multiple_of(jnp.where(step < 0, 32, 62 * 16), 16), SLOT), :]
    for copy in stores:
        copy.wait()


def edge_kernel(side_ref, courant_ref, edge_ref, halo_ref, _, out_ref, raw, slot, sem):
    step = side_ref[0]
    raw[32:96, :] = edge_ref[...]
    at = pl.multiple_of(jnp.where(step < 0, 0, 96), 16)
    for j in range(16):
        raw[pl.ds(at + j, 2, stride=16), :] = halo_ref[:, 128 * j : 128 * j + 128]

    def store(cell, half, value):
        slot[pl.ds(2 * cell + half, 8, stride=8), :] = value

    sweeps(raw, 4, 32, step, courant_ref, store)
    copy = pltpu.make_async_copy(slot, out_ref.at[jnp.where(step < 0, THERE_AT[0], THERE_AT[15])], sem)
    copy.start()
    copy.wait()


def tables_kernel(
    where_ref, order_ref, kern_ref, const_ref, base_ref, ks_ref, mask_ref, rows, turned
):
    position = lax.broadcasted_iota(jnp.int32, (1, 64), 1)
    first = position < BLOCK_CELLS * where_ref[1]
    for c in range(4):
        hit = jnp.where(first & (order_ref[...] == 4 * where_ref[0] + c), STEP_SCALE, 0.0)
        mask_ref[2 * c : 2 * c + 2, :] = jnp.broadcast_to(jnp.sum(hit, axis=1, keepdims=True), (2, 128))
    base_ref[...] = const_ref[0:576, :]
    for kx in range(32):
        for ch in range(8):
            at = kx * 8 + ch
            back = ((32 - kx) % 32) * 8 + ch
            tile = kern_ref[:, at * 128 : at * 128 + 128]
            rows[pl.ds(at, KERN, stride=256), :] = tile
            turned[pl.ds(back, KERN, stride=256), :] = tile
    group = lax.broadcasted_iota(jnp.int32, (32, 128), 1) // 32

    def ordered(src, t, k8):
        g, h = k8 % 4, k8 // 4
        out = None
        for k4 in range(4):
            piece = src[pl.ds(t * 256 + 2 * k4 + h, 32, stride=8), :]
            if k4 != g:
                piece = pltpu.roll(piece, ((k4 - g) % 4) * 32, 1)
            out = piece if out is None else jnp.where(group == k4, piece, out)
        return out

    scale = 0.5 / NV**3
    for k8 in range(8):
        at = 576 if k8 == 0 else 704
        flip = const_ref[at : at + 128, :].astype(BF16)
        for t in range(KERN):
            straight = ordered(rows, t, k8)
            other = ordered(turned, t, (8 - k8) % 8)
            hi, lo = split(other)
            ks_ref[k8, t] = scale * (straight + (dot(hi, flip) + dot(lo, flip)))


def turn(k8, lane_y4):
    cvec = jnp.full((1, 128), 1.0, F32)
    svec = jnp.full((1, 128), 0.0, F32)
    for y4 in range(1, 4):
        angle = 2 * math.pi * y4 * k8 / 32
        cvec = jnp.where(lane_y4 == y4, math.cos(angle), cvec)
        svec = jnp.where(lane_y4 == y4, math.sin(angle), svec)
    return cvec, svec


ROOT = math.sqrt(0.5)
PAIRS = ((0, 4), (1, 7), (2, 6), (3, 5))


def forward8(x):
    a = [x[j] + x[j + 4] for j in range(4)]
    d = [x[j] - x[j + 4] for j in range(4)]
    even, odd = a[0] + a[2], a[1] + a[3]
    less, more = ROOT * (d[1] - d[3]), ROOT * (d[1] + d[3])
    return (
        (even + odd, even - odd),
        (d[0] + less, -d[2] - more),
        (a[0] - a[2], a[3] - a[1]),
        (d[0] - less, d[2] - more),
    )


def inverse8(r0, r4, c1, s1, c2, s2, c3, s3):
    e, o = r0 + r4, r0 - r4
    a, b, c, d = e + c2, e - c2, c1 + c3, s3 - s1
    p, q = o - s2, o + s2
    less, more = ROOT * (c1 - c3), ROOT * (s1 + s3)
    m, n = less - more, less + more
    return [a + c, p + m, b + d, q - n, a - c, p - m, b - d, q + n]


def right(base_ref, k8, inverse):
    c, s = base_ref[0:128, :], base_ref[128:256, :]
    if k8:
        cvec, svec = turn(k8, lax.broadcasted_iota(jnp.int32, (1, 128), 1) // 32)
        c, s = cvec * c - svec * s, cvec * s + svec * c
    halves = []
    for c, s in zip(split(c), split(s)):
        up, down = (s, -s) if inverse else (-s, s)
        halves.append(
            jnp.concatenate(
                [jnp.concatenate([c, up], axis=1), jnp.concatenate([down, c], axis=1)], axis=0
            )
        )
    return halves


def left_matrices(base_ref, lf_ref, li_ref):
    zero = jnp.zeros((32, 128), BF16)
    c, s = base_ref[256:288, :], base_ref[288:320, :]
    cell = (lax.broadcasted_iota(jnp.int32, (32, 128), 1) % 8) // 2
    for p in range(2):
        first, second = cell == 2 * p, cell == 2 * p + 1
        real = split(jnp.where(first, c, jnp.where(second, s, 0.0)))
        imag = split(jnp.where(first, -s, jnp.where(second, c, 0.0)))
        for half in range(2):
            re, im = real[half], imag[half]
            for kk in range(2):
                at = 128 * kk + 64 * p
                top, low = slice(at, at + 32), slice(at + 32, at + 64)
                mine, other = slice(128 * kk, 128 * kk + 128), slice(128 - 128 * kk, 256 - 128 * kk)
                lf_ref[0, half, top, mine], lf_ref[0, half, low, mine] = re, im
                lf_ref[0, half, top, other], lf_ref[0, half, low, other] = zero, zero
                lf_ref[1, half, top, 0:128], lf_ref[1, half, low, 0:128] = re, im
                lf_ref[1, half, top, 128:256] = im if kk else -im
                lf_ref[1, half, low, 128:256] = -re if kk else re
    zero = jnp.zeros((128, 128), BF16)
    c, s = base_ref[320:448, :], base_ref[448:576, :]
    cell = (lax.broadcasted_iota(jnp.int32, (128, 128), 0) % 8) // 2
    lane = lax.broadcasted_iota(jnp.int32, (128, 128), 1)
    first, second = cell == 2 * (lane // 64), cell == 2 * (lane // 64) + 1
    real = (lane // 32) % 2 == 0
    zeroth = split(jnp.where(first, jnp.where(real, c, -s), jnp.where(second, jnp.where(real, s, c), 0.0)))
    other = split(jnp.where(first, jnp.where(real, s, c), jnp.where(second, jnp.where(real, -c, s), 0.0)))
    for half in range(2):
        a, b = zeroth[half], other[half]
        up, low = slice(0, 128), slice(128, 256)
        li_ref[0, half, up, up], li_ref[0, half, up, low] = a, zero
        li_ref[0, half, low, up], li_ref[0, half, low, low] = zero, a
        li_ref[1, half, up, up], li_ref[1, half, up, low] = a, a
        li_ref[1, half, low, up], li_ref[1, half, low, low] = b, -b


def collide_kernel(
    x_ref, base_ref, ks_ref, mask_ref, out_ref, lf_ref, li_ref, fh, fl, y, gh, gl, spec, mh, ml, back
):
    left_matrices(base_ref, lf_ref, li_ref)
    for v in range(0, 16, 2):
        x = [
            jnp.concatenate(
                [x_ref[THERE_AT[v + i], 8 * ch : 8 * ch + 8, :] for i in range(2)], axis=0
            )
            for ch in range(8)
        ]
        for g, parts in enumerate(forward8(x)):
            for u, part in enumerate(parts):
                rows, lanes = slice(128 * u + 8 * v, 128 * u + 8 * v + 16), slice(128 * g, 128 * g + 128)
                fh[rows, lanes], fl[rows, lanes] = split(part)
    for i, lanes in enumerate((slice(0, 128), slice(128, 512))):
        y[:, lanes] = dot3(lf_ref[i, 0], lf_ref[i, 1], fh[:, lanes], fl[:, lanes])
    lane_y4 = lax.broadcasted_iota(jnp.int32, (1, 128), 1) // 32
    for g in range(4):
        for kk in range(2):
            k8 = PAIRS[g][kk]
            cvec, svec = turn(k8, lane_y4)
            for p in range(2):
                at = 128 * kk + 64 * p
                lanes = slice(128 * g, 128 * g + 128)
                re, im = y[at : at + 32, lanes], y[at + 32 : at + 64, lanes]
                if k8:
                    re, im = re * cvec + im * svec, im * cvec - re * svec
                rows = slice(64 * k8 + 32 * p, 64 * k8 + 32 * p + 32)
                gh[rows, 0:128], gl[rows, 0:128] = split(re)
                gh[rows, 128:256], gl[rows, 128:256] = split(im)
    spec[...] = dot3(gh[...], gl[...], *right(base_ref, 0, False))
    for g in range(4):
        for kk in range(2):
            k8 = PAIRS[g][kk]
            parts = []
            for t in range(KERN):
                ks = ks_ref[k8, t]
                ks = jnp.concatenate([ks, ks], axis=1)
                for p in range(2):
                    at = 64 * k8 + 32 * p
                    parts.append(spec[at : at + 32, :] * ks)
            hi, lo = split(jnp.concatenate(parts, axis=0))
            done = dot3(hi, lo, *right(base_ref, k8, True))
            hi, lo = split(done)
            for n in range(2 * KERN):
                t, p = n // 2, n % 2
                lanes = slice(128 * (KERN * g + t), 128 * (KERN * g + t) + 128)
                for ri in range(2):
                    at = 128 * kk + 64 * p + 32 * ri
                    part = (slice(32 * n, 32 * n + 32), slice(128 * ri, 128 * ri + 128))
                    mh[at : at + 32, lanes] = hi[part]
                    ml[at : at + 32, lanes] = lo[part]
    for i, lanes in enumerate((slice(0, 640), slice(640, 2560))):
        back[:, lanes] = dot3(li_ref[i, 0], li_ref[i, 1], mh[:, lanes], ml[:, lanes])
    mask = mask_ref[...]
    for v in range(16):
        def part(t):
            parts = []
            for g in range(4):
                lanes = slice(128 * (KERN * g + t), 128 * (KERN * g + t) + 128)
                for u in range(2):
                    parts.append(back[128 * u + 8 * v : 128 * u + 8 * v + 8, lanes])
            return inverse8(*parts)

        total = [a * b for a, b in zip(part(0), part(1))]
        total = [a + b * c for a, b, c in zip(total, part(2), part(3))]
        for ch, (gain, loss) in enumerate(zip(total, part(4))):
            f = x_ref[THERE_AT[v], 8 * ch : 8 * ch + 8, :]
            out_ref[BACK_AT[v], 8 * ch : 8 * ch + 8, :] = f + mask * (gain - f * loss)


def place_kernel(in_ref, out_ref, out, sem):
    stores = [
        pltpu.make_async_copy(out.at[pl.ds(8 * i, 8)], out_ref.at[pl.ds(8 * i, 8)], sem.at[i])
        for i in range(8)
    ]
    for tile in range(8):
        for x2 in range(2):
            for ch in range(8):
                j = 8 * x2 + ch
                for k in range(2):
                    at = BACK_AT[2 * tile + k] * SLOT + 8 * ch + x2
                    out[8 * tile + 4 * k : 8 * tile + 4 * k + 4, 128 * j : 128 * j + 128] = in_ref[
                        pl.ds(at, 4, stride=2), :
                    ]
        stores[tile].start()
    for copy in stores:
        copy.wait()


VM = pl.BlockSpec(memory_space=pltpu.VMEM)
SM = pl.BlockSpec(memory_space=pltpu.SMEM)
ANY = pl.BlockSpec(memory_space=pl.ANY)


def shape(*dims, dtype=F32):
    return jax.ShapeDtypeStruct(dims, dtype)


def params(mib):
    return pltpu.CompilerParams(vmem_limit_bytes=mib << 20)


def transport(side, courant, dist):
    return pl.pallas_call(
        transport_kernel,
        out_shape=[shape(16, SLOT, 128), shape(SLOT, 128)],
        in_specs=[SM, SM, VM],
        out_specs=[ANY, VM],
        scratch_shapes=[
            pltpu.VMEM((68 * 16, 128), F32),
            pltpu.VMEM((16, SLOT, 128), F32),
            pltpu.SemaphoreType.DMA((16,)),
        ],
        compiler_params=params(8),
        cost_estimate=pl.CostEstimate(flops=4000000, bytes_accessed=1 << 20, transcendentals=0),
        name="transport",
    )(side, courant, dist)


def edges(side, courant, edge, halo, mine):
    return pl.pallas_call(
        edge_kernel,
        out_shape=shape(16, SLOT, 128),
        in_specs=[SM, SM, VM, VM, ANY],
        out_specs=ANY,
        input_output_aliases={4: 0},
        scratch_shapes=[
            pltpu.VMEM((128, 128), F32),
            pltpu.VMEM((SLOT, 128), F32),
            pltpu.SemaphoreType.DMA,
        ],
        compiler_params=params(8),
        name="edges",
    )(side, courant, edge, halo, mine)


def make_tables(where, order, kernels):
    rows = pltpu.VMEM((KERN * 256, 128), F32)
    return pl.pallas_call(
        tables_kernel,
        out_shape=[shape(576, 128), shape(8, KERN, 32, 128), shape(8, 128)],
        in_specs=[SM] + [VM] * 3,
        out_specs=[VM] * 3,
        scratch_shapes=[rows, rows],
        compiler_params=params(12),
        cost_estimate=pl.CostEstimate(flops=8000000, bytes_accessed=4 << 20, transcendentals=0),
        name="tables",
    )(where, order, kernels, jnp.asarray(constant_rows()))


def collide(x, tables):
    left = pltpu.VMEM((2, 2, 256, 256), BF16)
    half = pltpu.VMEM((256, 512), BF16)
    field = pltpu.VMEM((512, 256), BF16)
    wide = pltpu.VMEM((256, 2560), BF16)
    return pl.pallas_call(
        collide_kernel,
        out_shape=shape(16, SLOT, 128),
        in_specs=[VM] * 4,
        out_specs=VM,
        scratch_shapes=[
            left,
            left,
            half,
            half,
            pltpu.VMEM((256, 512), F32),
            field,
            field,
            pltpu.VMEM((512, 256), F32),
            wide,
            wide,
            pltpu.VMEM((256, 2560), F32),
        ],
        compiler_params=params(20),
        name="collide",
    )(x, *tables)


def place(x):
    return pl.pallas_call(
        place_kernel,
        out_shape=shape(64, 2048),
        in_specs=[VM],
        out_specs=ANY,
        scratch_shapes=[pltpu.VMEM((64, 2048), F32), pltpu.SemaphoreType.DMA((8,))],
        compiler_params=params(8),
        name="place",
    )(x.reshape(16 * SLOT, 128))


def exchange(slots, order):
    return lax.all_to_all(
        slots, "vel", split_axis=0, concat_axis=0, tiled=True, axis_index_groups=[list(order)]
    )


def local(distribution, collision_order, collision_blocks, kernels):
    v = lax.axis_index("vel")
    rising = v >= 8
    x = 2 * v + lax.iota(jnp.int32, 2)
    courant = jnp.abs(COURANT_MAX * (2.0 * x.astype(F32) - (NV - 1)) / (NV - 1))
    side = jnp.where(rising, -1, 1).astype(jnp.int32)[None]
    pairs = []
    for s in range(16):
        for u in range(16):
            to = s + 1 if u >= 8 else s - 1
            if 0 <= to < 16:
                pairs.append((s * 16 + u, to * 16 + u))
    send = jnp.where(rising, distribution[62:64], distribution[0:2])
    mine, edge = transport(side, courant, distribution)
    halo = lax.ppermute(send, ("space", "vel"), pairs)
    mine = edges(side, courant, edge, halo, mine)
    where = jnp.stack([v.astype(jnp.int32), collision_blocks[0]])
    tables = make_tables(where, collision_order, kernels)
    cells = exchange(mine, THERE)
    return place(exchange(collide(cells, tables), BACK))


def solution(mesh):
    in_specs = (P("space", "vel"), P("space", None), P("space"), P())
    out_specs = P("space", "vel")
    return jax.shard_map(local, mesh=mesh, in_specs=in_specs, out_specs=out_specs, check_vma=False)
```

time: 50.9 us -> 44.6 us (0.88)
  Pallas kernels: 14 us -> 9.78 us
  waiting for transfers between devices: 6.53 us -> 4.67 us
  starting transfers between devices: 9.36 us -> 11.1 us
  blocking collectives: 16.2 us -> 15.2 us
  local copies, waits for them, and re-layouts: 2.57 us -> 1.62 us
    pallas_call x2, Pallas kernels: 10.3 us -> 6.06 us  [the longest x1 3.64 us: collide(): pl.pallas_call(collide_kernel, out_shape=shape(16, SLOT, 128), in_specs=[...]
    all_to_all x1, waiting for transfers between devices: 6.52 us -> 4.66 us  [exchange(): lax.all_to_all(slots, 'vel', split_axis=0, concat_axis=0, tiled=True, axi...]
    all_to_all x1, starting transfers between devices: 7.44 us -> 9.18 us  [exchange(): lax.all_to_all(slots, 'vel', split_axis=0, concat_axis=0, tiled=True, axi...]
    all_to_all x1, blocking collectives: 16.2 us -> 15.2 us  [exchange(): lax.all_to_all(slots, 'vel', split_axis=0, concat_axis=0, tiled=True, axi...]
    unnamed x8, local copies, waits for them, and re-layouts: 2.57 us -> 1.62 us
where the time goes in v2:
time: 44.6 us; the launch traced here: 44 us
  blocking collectives  15.2 us (34%)
  starting transfers between devices  11.1 us (25%)
  Pallas kernels  9.78 us (22%)
  waiting for transfers between devices  4.67 us (10%)
  local copies, waits for them, and re-layouts  1.62 us (4%)
  other arithmetic  0.97 us (2%)
  between operations  0.75 us (2%)
    all_to_all x1, blocking collectives, exchange(): lax.all_to_all(slots, 'vel', split_axis=0, concat_axis=0, tiled=True, axi...  15.2 us
    all_to_all x1, starting transfers between devices, exchange(): lax.all_to_all(slots, 'vel', split_axis=0, concat_axis=0, tiled=True, axi...  9.18 us
    all_to_all x1, waiting for transfers between devices, exchange(): lax.all_to_all(slots, 'vel', split_axis=0, concat_axis=0, tiled=True, axi...  4.66 us
    pallas_call x1, Pallas kernels, collide(): pl.pallas_call(collide_kernel, out_shape=shape(16, SLOT, 128), in_specs=[...  3.64 us
    pallas_call x1, Pallas kernels, make_tables(): pl.pallas_call(tables_kernel, out_shape=[shape(576, 128), shape(8, KERN,...  2.41 us
    ppermute x1, starting transfers between devices, local(): halo = lax.ppermute(send, ('space', 'vel'), pairs)  1.92 us
    pallas_call x1, Pallas kernels, transport(): pl.pallas_call(transport_kernel, out_shape=[shape(16, SLOT, 128), shape(S...  1.66 us
    unnamed x8, local copies, waits for them, and re-layouts  1.62 us
  transfers between devices with their start and end apart: 2, of which 1 were waited for; matrix products, arithmetic and copies ran while one was open for 0% of the time, Pallas kernels for 9%

profile of v2, /device:TPU:96, one launch (start us, length us, event | category | flops | bytes accessed | tf_op | source)
XLA Modules:
  0.0 44.0 jit_solution(15159021496186674032)
XLA Ops:
  0.0 0.9 %slice_select_fusion = f32[2,2048]{1,0:T(2,128)S(1)} fusion(f32[64,2048]{1,0:T(8,128)} %dist_ref.1, pred[]{:T(512)S(6)} %ge.3), kind=kLoop, calls=%fused_computation | loop fusion | flops 4096 | bytes 49153 | tf_op jit(solution)/shard_map/jit(_where)/select_n | solution.py:452
  0.9 1.9 %collective-permute-start = (f32[2,2048]{1,0:T(2,128)S(1)}, f32[2,2048]{1,0:T(2,128)S(1)}, u32[]{:S(2)}, u32[]{:S(2)}) collective-permute-start(f32[2,2048]{1,0:T(2,128)S(1)} %slice_select_fusion), channel_id=1, source_target_pairs={{8,24},{9,25},{10,26},{11,27},{12,28},{13,29},{14,30},{15,31},{16,... | collective-permute-start | bytes 49160 | tf_op jit(solution)/shard_map/ppermute | solution.py:454
  2.8 0.0 copy-start.1
  2.8 1.0 %copy-done.1 = f32[64,2048]{1,0:T(8,128)S(1)} copy-done((f32[64,2048]{1,0:T(8,128)S(1)}, f32[64,2048]{1,0:T(8,128)}, u32[]{:S(2)}) %copy-start.1) | copy-done | bytes 524312
  3.9 1.7 %transport.1 = (f32[16,64,128]{2,1,0:T(8,128)}, f32[64,128]{1,0:T(8,128)S(1)}) custom-call(s32[1]{0:T(128)} %bitcast.side_ref, f32[2]{0:T(128)S(1)} %multiply_abs_fusion.courant_ref, f32[64,2048]{1,0:T(8,128)S(1)} %copy-done.1), custom_call_target="tpu_custom_call" | custom-call | flops 4000000 | bytes 1048576 | tf_op jit(solution)/shard_map/transport/pallas_call | solution.py:347
  5.5 0.0 collective-permute-done.halo_ref
  5.6 0.0 copy-start
  5.6 1.2 %edges.1 = f32[16,64,128]{2,1,0:T(8,128)} custom-call(s32[1]{0:T(128)} %bitcast.side_ref, f32[2]{0:T(128)S(1)} %multiply_abs_fusion.courant_ref, f32[64,128]{1,0:T(8,128)S(1)} %get-tuple-element.10.edge_ref, f32[2,2048]{1,0:T(2,128)S(1)} %collective-permute-done.halo_ref, f32[16,64,128]{2,1,0:T(8,128)} %get-tuple-element.11._), custom_call_target="tpu_custom_call", output_to_operand_aliasing={{}: (4, {})} | custom-call | tf_op jit(solution)/shard_map/edges/pallas_call | solution.py:364
  6.8 0.0 copy-start.2
  6.8 9.2 %all-to-all-start = ((f32[16,64,128]{2,1,0:T(8,128)}), f32[16,64,128]{2,1,0:T(8,128)S(1)}, u32[]{:S(2)}, u32[]{:S(2)}) async-start(f32[16,64,128]{2,1,0:T(8,128)} %edges.1), calls=%async_computation | async-start | bytes 1048576 | tf_op jit(solution)/shard_map/all_to_all | solution.py:435
  16.6 0.0 copy-start.3
  16.6 0.1 pad_add_fusion.where_ref
  16.7 0.0 copy-done
  16.7 0.0 copy-done.2
  16.7 0.6 %copy-done.3 = s32[1,64]{1,0:T(1,128)S(1)} copy-done((s32[1,64]{1,0:T(1,128)S(1)}, s32[1,64]{1,0:T(1,128)}, u32[]{:S(2)}) %copy-start.3) | copy-done | bytes 280
  17.3 2.4 %tables.1 = (f32[576,128]{1,0:T(8,128)S(1)}, f32[8,5,32,128]{3,2,1,0:T(8,128)S(1)}, f32[8,128]{1,0:T(8,128)S(1)}) custom-call(s32[2]{0:T(128)S(1)} %pad_add_fusion.where_ref, s32[1,64]{1,0:T(1,128)S(1)} %copy-done.3, f32[5,32768]{1,0:T(8,128)S(1)} %copy-done, f32[832,128]{1,0:T(8,128)S(1)} %copy-done.2), custom_call_target="tpu_custom_call" | custom-call | flops 8000000 | bytes 4194304 | tf_op jit(solution)/shard_map/tables/pallas_call | solution.py:382
  19.7 4.7 %all-to-all-done.x_ref = f32[16,64,128]{2,1,0:T(8,128)S(1)} async-done(((f32[16,64,128]{2,1,0:T(8,128)}), f32[16,64,128]{2,1,0:T(8,128)S(1)}, u32[]{:S(2)}, u32[]{:S(2)}) %all-to-all-start) | async-done | bytes 524320 | tf_op jit(solution)/shard_map/all_to_all | solution.py:435
  24.4 3.6 %collide.1 = f32[16,64,128]{2,1,0:T(8,128)S(1)} custom-call(f32[16,64,128]{2,1,0:T(8,128)S(1)} %all-to-all-done.x_ref, f32[576,128]{1,0:T(8,128)S(1)} %get-tuple-element.12.base_ref, f32[8,5,32,128]{3,2,1,0:T(8,128)S(1)} %get-tuple-element.13.ks_ref, f32[8,128]{1,0:T(8,128)S(1)} %get-tuple-element.14.mask_ref), custom_call_target="tpu_custom_call" | custom-call | tf_op jit(solution)/shard_map/collide/pallas_call | solution.py:399
  28.0 15.2 %all_to_all.10 = f32[16,64,128]{2,1,0:T(8,128)S(1)} all-to-all(f32[16,64,128]{2,1,0:T(8,128)S(1)} %collide.1), channel_id=1, replica_groups={{15,14,13,12,11,10,9,8,7,6,5,4,3,2,1,0},{31,30,29,28,27,26,25,24,23,22,..., dimensions={0} | all-to-all | bytes 1048576 | tf_op jit(solution)/shard_map/all_to_all | solution.py:435
  43.2 0.9 %place.1 = f32[64,2048]{1,0:T(8,128)} custom-call(f32[1024,128]{1,0:T(8,128)S(1)} %bitcast.3), custom_call_target="tpu_custom_call" | custom-call | tf_op jit(solution)/shard_map/place/pallas_call | solution.py:423
  (1 shorter events, 0.0 us)
Async XLA Ops:
  0.9 4.7 %collective-permute-start = (f32[2,2048]{1,0:T(2,128)S(1)}, f32[2,2048]{1,0:T(2,128)S(1)}, u32[]{:S(2)}, u32[]{:S(2)}) collective-permute-start(f32[2,2048]{1,0:T(2,128)S(1)} %slice_select_fusion), channel_id=1, source_target_pairs={{8,24},{9,25},{10,26},{11,27},{12,28},{13,29},{14,30},{15,31},{16,... | collective-permute-start | bytes 49160 | tf_op jit(solution)/shard_map/ppermute | solution.py:454
  2.8 1.0 %copy-start.1 = (f32[64,2048]{1,0:T(8,128)S(1)}, f32[64,2048]{1,0:T(8,128)}, u32[]{:S(2)}) copy-start(f32[64,2048]{1,0:T(8,128)} %dist_ref.1) | copy-start | bytes 1572868
  5.6 11.1 %copy-start = (f32[5,32768]{1,0:T(8,128)S(1)}, f32[5,32768]{1,0:T(8,128)}, u32[]{:S(2)}) copy-start(f32[5,32768]{1,0:T(8,128)} %kern_ref.1) | copy-start | bytes 1966084
  6.8 9.9 %copy-start.2 = (f32[832,128]{1,0:T(8,128)S(1)}, f32[832,128]{1,0:T(8,128)}, u32[]{:S(2)}) copy-start(f32[832,128]{1,0:T(8,128)} %constant.23.clone.const_ref) | copy-start | bytes 1277956
  6.8 17.6 %all-to-all-start = ((f32[16,64,128]{2,1,0:T(8,128)}), f32[16,64,128]{2,1,0:T(8,128)S(1)}, u32[]{:S(2)}, u32[]{:S(2)}) async-start(f32[16,64,128]{2,1,0:T(8,128)} %edges.1), calls=%async_computation | async-start | bytes 1048576 | tf_op jit(solution)/shard_map/all_to_all | solution.py:435
  16.6 0.7 %copy-start.3 = (s32[1,64]{1,0:T(1,128)S(1)}, s32[1,64]{1,0:T(1,128)}, u32[]{:S(2)}) copy-start(s32[1,64]{1,0:T(1,128)} %order_ref.1) | copy-start | bytes 772

commit v3 on v2

--- a/solution.py
+++ b/solution.py
@@ -17,8 +17,8 @@
 BF16 = jnp.bfloat16
 SLOT = 64
 
-THERE = (15, 14, 13, 12, 11, 10, 9, 8, 7, 6, 5, 4, 3, 2, 1, 0)
-BACK = (15, 14, 13, 12, 11, 10, 9, 8, 7, 6, 5, 4, 3, 2, 1, 0)
+THERE = (10, 11, 14, 15, 9, 13, 6, 7, 5, 8, 12, 2, 3, 1, 4, 0)
+BACK = (10, 15, 5, 0, 11, 14, 4, 1, 9, 12, 6, 3, 8, 13, 7, 2)
 THERE_AT = [THERE.index(v) for v in range(16)]
 BACK_AT = [BACK.index(v) for v in range(16)]
 
@@ -239,8 +239,13 @@
         li_ref[1, half, low, up], li_ref[1, half, low, low] = b, -b
 
 
+def columns(g, t):
+    at = 128 * (t if g == 0 else KERN + 3 * t + g - 1)
+    return slice(at, at + 128)
+
+
 def collide_kernel(
-    x_ref, base_ref, ks_ref, mask_ref, out_ref, lf_ref, li_ref, fh, fl, y, gh, gl, spec, mh, ml, back
+    x_ref, base_ref, ks_ref, mask_ref, out_ref, lf_ref, li_ref, fh, fl, y, gh, gl, spec, mh, ml, back, total
 ):
     left_matrices(base_ref, lf_ref, li_ref)
     for v in range(0, 16, 2):
@@ -286,29 +291,39 @@
             hi, lo = split(done)
             for n in range(2 * KERN):
                 t, p = n // 2, n % 2
-                lanes = slice(128 * (KERN * g + t), 128 * (KERN * g + t) + 128)
                 for ri in range(2):
                     at = 128 * kk + 64 * p + 32 * ri
                     part = (slice(32 * n, 32 * n + 32), slice(128 * ri, 128 * ri + 128))
-                    mh[at : at + 32, lanes] = hi[part]
-                    ml[at : at + 32, lanes] = lo[part]
-    for i, lanes in enumerate((slice(0, 640), slice(640, 2560))):
+                    mh[at : at + 32, columns(g, t)] = hi[part]
+                    ml[at : at + 32, columns(g, t)] = lo[part]
+
+    def over_x(i, lanes):
         back[:, lanes] = dot3(li_ref[i, 0], li_ref[i, 1], mh[:, lanes], ml[:, lanes])
+
+    def values(v, t):
+        parts = [
+            back[128 * u + 8 * v : 128 * u + 8 * v + 8, columns(g, t)]
+            for g in range(4)
+            for u in range(2)
+        ]
+        return inverse8(*parts)
+
+    over_x(0, slice(0, 128 * KERN))
+    over_x(1, slice(columns(1, 0).start, columns(3, 1).stop))
+    for v in range(16):
+        for ch, (a, b) in enumerate(zip(values(v, 0), values(v, 1))):
+            total[v, 8 * ch : 8 * ch + 8, :] = a * b
+    over_x(1, slice(columns(1, 2).start, columns(3, 3).stop))
+    for v in range(16):
+        for ch, (a, b) in enumerate(zip(values(v, 2), values(v, 3))):
+            total[v, 8 * ch : 8 * ch + 8, :] = total[v, 8 * ch : 8 * ch + 8, :] + a * b
+    over_x(1, slice(columns(1, 4).start, columns(3, 4).stop))
     mask = mask_ref[...]
     for v in range(16):
-        def part(t):
-            parts = []
-            for g in range(4):
-                lanes = slice(128 * (KERN * g + t), 128 * (KERN * g + t) + 128)
-                for u in range(2):
-                    parts.append(back[128 * u + 8 * v : 128 * u + 8 * v + 8, lanes])
-            return inverse8(*parts)
-
-        total = [a * b for a, b in zip(part(0), part(1))]
-        total = [a + b * c for a, b, c in zip(total, part(2), part(3))]
-        for ch, (gain, loss) in enumerate(zip(total, part(4))):
-            f = x_ref[THERE_AT[v], 8 * ch : 8 * ch + 8, :]
-            out_ref[BACK_AT[v], 8 * ch : 8 * ch + 8, :] = f + mask * (gain - f * loss)
+        for ch, loss in enumerate(values(v, 4)):
+            rows = slice(8 * ch, 8 * ch + 8)
+            f = x_ref[THERE_AT[v], rows, :]
+            out_ref[BACK_AT[v], rows, :] = f + mask * (total[v, rows, :] - f * loss)
 
 
 def place_kernel(in_ref, out_ref, out, sem):
@@ -413,6 +428,7 @@
             wide,
             wide,
             pltpu.VMEM((256, 2560), F32),
+            pltpu.VMEM((16, SLOT, 128), F32),
         ],
         compiler_params=params(20),
         name="collide",

time: 44.6 us -> 43.7 us (0.980)
  the two profiles are of different devices: /device:TPU:96 before, /device:TPU:1 now
where the time goes in v3:
time: 43.7 us; the launch traced here: 43.3 us
  blocking collectives  14.2 us (32%)
  starting transfers between devices  13.9 us (32%)
  Pallas kernels  9.76 us (22%)
  waiting for transfers between devices  2.14 us (5%)
  local copies, waits for them, and re-layouts  1.62 us (4%)
  other arithmetic  0.97 us (2%)
  between operations  0.75 us (2%)
    all_to_all x1, blocking collectives, exchange(): lax.all_to_all(slots, 'vel', split_axis=0, concat_axis=0, tiled=True, axi...  14.2 us
    all_to_all x1, starting transfers between devices, exchange(): lax.all_to_all(slots, 'vel', split_axis=0, concat_axis=0, tiled=True, axi...  8.79 us
    ppermute x1, starting transfers between devices, local(): halo = lax.ppermute(send, ('space', 'vel'), pairs)  5.11 us
    pallas_call x1, Pallas kernels, collide(): pl.pallas_call(collide_kernel, out_shape=shape(16, SLOT, 128), in_specs=[...  3.63 us
    pallas_call x1, Pallas kernels, make_tables(): pl.pallas_call(tables_kernel, out_shape=[shape(576, 128), shape(8, KERN,...  2.41 us
    all_to_all x1, waiting for transfers between devices, exchange(): lax.all_to_all(slots, 'vel', split_axis=0, concat_axis=0, tiled=True, axi...  2.13 us
    pallas_call x1, Pallas kernels, transport(): pl.pallas_call(transport_kernel, out_shape=[shape(16, SLOT, 128), shape(S...  1.65 us
    unnamed x8, local copies, waits for them, and re-layouts  1.62 us
  transfers between devices with their start and end apart: 2, of which 1 were waited for; matrix products, arithmetic and copies ran while one was open for 0% of the time, Pallas kernels for 9%

profile of v3, /device:TPU:1, one launch (start us, length us, event | category | flops | bytes accessed | tf_op | source)
XLA Modules:
  0.0 43.3 jit_solution(14422962564938297545)
XLA Ops:
  0.0 0.9 %slice_select_fusion = f32[2,2048]{1,0:T(2,128)S(1)} fusion(f32[64,2048]{1,0:T(8,128)} %dist_ref.1, pred[]{:T(512)S(6)} %ge.3), kind=kLoop, calls=%fused_computation | loop fusion | flops 4096 | bytes 49153 | tf_op jit(solution)/shard_map/jit(_where)/select_n | solution.py:468
  0.9 5.1 %collective-permute-start = (f32[2,2048]{1,0:T(2,128)S(1)}, f32[2,2048]{1,0:T(2,128)S(1)}, u32[]{:S(2)}, u32[]{:S(2)}) collective-permute-start(f32[2,2048]{1,0:T(2,128)S(1)} %slice_select_fusion), channel_id=1, source_target_pairs={{8,24},{9,25},{10,26},{11,27},{12,28},{13,29},{14,30},{15,31},{16,... | collective-permute-start | bytes 49160 | tf_op jit(solution)/shard_map/ppermute | solution.py:470
  6.0 0.0 copy-start.1
  6.0 1.0 %copy-done.1 = f32[64,2048]{1,0:T(8,128)S(1)} copy-done((f32[64,2048]{1,0:T(8,128)S(1)}, f32[64,2048]{1,0:T(8,128)}, u32[]{:S(2)}) %copy-start.1) | copy-done | bytes 524312
  7.1 1.7 %transport.1 = (f32[16,64,128]{2,1,0:T(8,128)}, f32[64,128]{1,0:T(8,128)S(1)}) custom-call(s32[1]{0:T(128)} %bitcast.side_ref, f32[2]{0:T(128)S(1)} %multiply_abs_fusion.courant_ref, f32[64,2048]{1,0:T(8,128)S(1)} %copy-done.1), custom_call_target="tpu_custom_call" | custom-call | flops 4000000 | bytes 1048576 | tf_op jit(solution)/shard_map/transport/pallas_call | solution.py:362
  8.7 0.0 collective-permute-done.halo_ref
  8.7 0.0 copy-start
  8.8 1.2 %edges.1 = f32[16,64,128]{2,1,0:T(8,128)} custom-call(s32[1]{0:T(128)} %bitcast.side_ref, f32[2]{0:T(128)S(1)} %multiply_abs_fusion.courant_ref, f32[64,128]{1,0:T(8,128)S(1)} %get-tuple-element.10.edge_ref, f32[2,2048]{1,0:T(2,128)S(1)} %collective-permute-done.halo_ref, f32[16,64,128]{2,1,0:T(8,128)} %get-tuple-element.11._), custom_call_target="tpu_custom_call", output_to_operand_aliasing={{}: (4, {})} | custom-call | tf_op jit(solution)/shard_map/edges/pallas_call | solution.py:379
  10.0 0.0 copy-start.2
  10.0 8.8 %all-to-all-start = ((f32[16,64,128]{2,1,0:T(8,128)}), f32[16,64,128]{2,1,0:T(8,128)S(1)}, u32[]{:S(2)}, u32[]{:S(2)}) async-start(f32[16,64,128]{2,1,0:T(8,128)} %edges.1), calls=%async_computation | async-start | bytes 1048576 | tf_op jit(solution)/shard_map/all_to_all | solution.py:451
  19.4 0.0 copy-start.3
  19.4 0.1 pad_add_fusion.where_ref
  19.5 0.0 copy-done
  19.5 0.0 copy-done.2
  19.5 0.6 %copy-done.3 = s32[1,64]{1,0:T(1,128)S(1)} copy-done((s32[1,64]{1,0:T(1,128)S(1)}, s32[1,64]{1,0:T(1,128)}, u32[]{:S(2)}) %copy-start.3) | copy-done | bytes 280
  20.1 2.4 %tables.1 = (f32[576,128]{1,0:T(8,128)S(1)}, f32[8,5,32,128]{3,2,1,0:T(8,128)S(1)}, f32[8,128]{1,0:T(8,128)S(1)}) custom-call(s32[2]{0:T(128)S(1)} %pad_add_fusion.where_ref, s32[1,64]{1,0:T(1,128)S(1)} %copy-done.3, f32[5,32768]{1,0:T(8,128)S(1)} %copy-done, f32[832,128]{1,0:T(8,128)S(1)} %copy-done.2), custom_call_target="tpu_custom_call" | custom-call | flops 8000000 | bytes 4194304 | tf_op jit(solution)/shard_map/tables/pallas_call | solution.py:397
  22.5 2.1 %all-to-all-done.x_ref = f32[16,64,128]{2,1,0:T(8,128)S(1)} async-done(((f32[16,64,128]{2,1,0:T(8,128)}), f32[16,64,128]{2,1,0:T(8,128)S(1)}, u32[]{:S(2)}, u32[]{:S(2)}) %all-to-all-start) | async-done | bytes 524320 | tf_op jit(solution)/shard_map/all_to_all | solution.py:451
  24.6 3.6 %collide.1 = f32[16,64,128]{2,1,0:T(8,128)S(1)} custom-call(f32[16,64,128]{2,1,0:T(8,128)S(1)} %all-to-all-done.x_ref, f32[576,128]{1,0:T(8,128)S(1)} %get-tuple-element.12.base_ref, f32[8,5,32,128]{3,2,1,0:T(8,128)S(1)} %get-tuple-element.13.ks_ref, f32[8,128]{1,0:T(8,128)S(1)} %get-tuple-element.14.mask_ref), custom_call_target="tpu_custom_call" | custom-call | tf_op jit(solution)/shard_map/collide/pallas_call | solution.py:414
  28.3 14.2 %all_to_all.10 = f32[16,64,128]{2,1,0:T(8,128)S(1)} all-to-all(f32[16,64,128]{2,1,0:T(8,128)S(1)} %collide.1), channel_id=1, replica_groups={{10,15,5,0,11,14,4,1,9,12,6,3,8,13,7,2},{26,31,21,16,27,30,20,17,25,28,..., dimensions={0} | all-to-all | bytes 1048576 | tf_op jit(solution)/shard_map/all_to_all | solution.py:451
  42.4 0.9 %place.1 = f32[64,2048]{1,0:T(8,128)} custom-call(f32[1024,128]{1,0:T(8,128)S(1)} %bitcast.3), custom_call_target="tpu_custom_call" | custom-call | tf_op jit(solution)/shard_map/place/pallas_call | solution.py:439
  (1 shorter events, 0.0 us)
Async XLA Ops:
  0.9 7.9 %collective-permute-start = (f32[2,2048]{1,0:T(2,128)S(1)}, f32[2,2048]{1,0:T(2,128)S(1)}, u32[]{:S(2)}, u32[]{:S(2)}) collective-permute-start(f32[2,2048]{1,0:T(2,128)S(1)} %slice_select_fusion), channel_id=1, source_target_pairs={{8,24},{9,25},{10,26},{11,27},{12,28},{13,29},{14,30},{15,31},{16,... | collective-permute-start | bytes 49160 | tf_op jit(solution)/shard_map/ppermute | solution.py:470
  6.0 1.0 %copy-start.1 = (f32[64,2048]{1,0:T(8,128)S(1)}, f32[64,2048]{1,0:T(8,128)}, u32[]{:S(2)}) copy-start(f32[64,2048]{1,0:T(8,128)} %dist_ref.1) | copy-start | bytes 1572868
  8.7 10.8 %copy-start = (f32[5,32768]{1,0:T(8,128)S(1)}, f32[5,32768]{1,0:T(8,128)}, u32[]{:S(2)}) copy-start(f32[5,32768]{1,0:T(8,128)} %kern_ref.1) | copy-start | bytes 1966084
  10.0 9.5 %copy-start.2 = (f32[832,128]{1,0:T(8,128)S(1)}, f32[832,128]{1,0:T(8,128)}, u32[]{:S(2)}) copy-start(f32[832,128]{1,0:T(8,128)} %constant.23.clone.const_ref) | copy-start | bytes 1277956
  10.0 14.7 %all-to-all-start = ((f32[16,64,128]{2,1,0:T(8,128)}), f32[16,64,128]{2,1,0:T(8,128)S(1)}, u32[]{:S(2)}, u32[]{:S(2)}) async-start(f32[16,64,128]{2,1,0:T(8,128)} %edges.1), calls=%async_computation | async-start | bytes 1048576 | tf_op jit(solution)/shard_map/all_to_all | solution.py:451
  19.4 0.7 %copy-start.3 = (s32[1,64]{1,0:T(1,128)S(1)}, s32[1,64]{1,0:T(1,128)}, u32[]{:S(2)}) copy-start(s32[1,64]{1,0:T(1,128)} %order_ref.1) | copy-start | bytes 772

commit v4 on v3

--- a/solution.py
+++ b/solution.py
@@ -17,7 +17,7 @@
 BF16 = jnp.bfloat16
 SLOT = 64
 
-THERE = (10, 11, 14, 15, 9, 13, 6, 7, 5, 8, 12, 2, 3, 1, 4, 0)
+THERE = (10, 11, 14, 15, 9, 13, 6, 7, 0, 8, 12, 2, 3, 1, 4, 5)
 BACK = (10, 15, 5, 0, 11, 14, 4, 1, 9, 12, 6, 3, 8, 13, 7, 2)
 THERE_AT = [THERE.index(v) for v in range(16)]
 BACK_AT = [BACK.index(v) for v in range(16)]
@@ -53,26 +53,18 @@
     return dot(ahi, bhi) + dot(ahi, blo) + dot(alo, bhi)
 
 
-def upwind(f0, f1, f2, a):
+def upwind(near, info_ref, half):
+    l2, l1, f0, r1, r2 = near
+    rising = info_ref[0:8, :] > 0.0
+    a = info_ref[8 + 8 * half : 16 + 8 * half, :]
+    f1 = jnp.where(rising, l1, r1)
+    f2 = jnp.where(rising, l2, r2)
     once = f0 - a * (f0 - f1)
     beside = f1 - a * (f1 - f2)
     return once - a * (once - beside)
 
 
-def sweeps(raw, cells, first, step, courant_ref, store):
-    for cell in range(cells):
-        for half in range(2):
-            here = first + cell * 16 + 8 * half
-            f0 = raw[pl.ds(here, 8), :]
-            f1 = raw[pl.ds(pl.multiple_of(here + 16 * step, 8), 8), :]
-            f2 = raw[pl.ds(pl.multiple_of(here + 32 * step, 8), 8), :]
-            store(cell, half, upwind(f0, f1, f2, courant_ref[half]))
-
-
-def transport_kernel(
-    side_ref, courant_ref, dist_ref, out_ref, edge_ref, raw, slots, out_sem
-):
-    step = side_ref[0]
+def transport_kernel(info_ref, dist_ref, out_ref, edge_ref, raw, slots, out_sem):
     zero = jnp.zeros((32, 128), F32)
     raw[0:32, :] = zero
     raw[66 * 16 : 68 * 16, :] = zero
@@ -84,32 +76,39 @@
     stores = [
         pltpu.make_async_copy(slots.at[i], out_ref.at[i], out_sem.at[i]) for i in range(16)
     ]
-
-    def store(cell, half, value):
-        slots[THERE_AT[cell // 4], pl.ds(2 * (cell % 4) + half, 8, stride=8), :] = value
-        if cell % 4 == 3 and half == 1:
+    for cell in range(64):
+        for half in range(2):
+            near = [raw[16 * (cell + k) + 8 * half : 16 * (cell + k) + 8 * half + 8, :] for k in range(5)]
+            slots[THERE_AT[cell // 4], pl.ds(2 * (cell % 4) + half, 8, stride=8), :] = upwind(
+                near, info_ref, half
+            )
+        if cell % 4 == 3:
             stores[THERE_AT[cell // 4]].start()
-
-    sweeps(raw, 64, 32, step, courant_ref, store)
-    edge_ref[...] = raw[pl.ds(pl.multiple_of(jnp.where(step < 0, 32, 62 * 16), 16), SLOT), :]
+    edge_ref[0:96, :] = raw[32:128, :]
+    edge_ref[96:192, :] = raw[60 * 16 : 66 * 16, :]
     for copy in stores:
         copy.wait()
 
 
-def edge_kernel(side_ref, courant_ref, edge_ref, halo_ref, _, out_ref, raw, slot, sem):
-    step = side_ref[0]
-    raw[32:96, :] = edge_ref[...]
-    at = pl.multiple_of(jnp.where(step < 0, 0, 96), 16)
+def edge_kernel(info_ref, edge_ref, halo_ref, _, out_ref, left, right, slots, sem):
+    left[32:128, :] = edge_ref[0:96, :]
+    right[0:96, :] = edge_ref[96:192, :]
     for j in range(16):
-        raw[pl.ds(at + j, 2, stride=16), :] = halo_ref[:, 128 * j : 128 * j + 128]
-
-    def store(cell, half, value):
-        slot[pl.ds(2 * cell + half, 8, stride=8), :] = value
-
-    sweeps(raw, 4, 32, step, courant_ref, store)
-    copy = pltpu.make_async_copy(slot, out_ref.at[jnp.where(step < 0, THERE_AT[0], THERE_AT[15])], sem)
-    copy.start()
-    copy.wait()
+        rows = halo_ref[:, 128 * j : 128 * j + 128]
+        left[pl.ds(j, 2, stride=16), :] = rows
+        right[pl.ds(96 + j, 2, stride=16), :] = rows
+    copies = []
+    for i, (raw, at) in enumerate(((left, THERE_AT[0]), (right, THERE_AT[15]))):
+        for cell in range(4):
+            for half in range(2):
+                near = [
+                    raw[16 * (cell + k) + 8 * half : 16 * (cell + k) + 8 * half + 8, :] for k in range(5)
+                ]
+                slots[i, pl.ds(2 * cell + half, 8, stride=8), :] = upwind(near, info_ref, half)
+        copies.append(pltpu.make_async_copy(slots.at[i], out_ref.at[at], sem.at[i]))
+        copies[-1].start()
+    for copy in copies:
+        copy.wait()
 
 
 def tables_kernel(
@@ -358,11 +357,11 @@
     return pltpu.CompilerParams(vmem_limit_bytes=mib << 20)
 
 
-def transport(side, courant, dist):
+def transport(info, dist):
     return pl.pallas_call(
         transport_kernel,
-        out_shape=[shape(16, SLOT, 128), shape(SLOT, 128)],
-        in_specs=[SM, SM, VM],
+        out_shape=[shape(16, SLOT, 128), shape(192, 128)],
+        in_specs=[VM, VM],
         out_specs=[ANY, VM],
         scratch_shapes=[
             pltpu.VMEM((68 * 16, 128), F32),
@@ -372,24 +371,25 @@
         compiler_params=params(8),
         cost_estimate=pl.CostEstimate(flops=4000000, bytes_accessed=1 << 20, transcendentals=0),
         name="transport",
-    )(side, courant, dist)
-
-
-def edges(side, courant, edge, halo, mine):
+    )(info, dist)
+
+
+def edges(info, edge, halo, mine):
     return pl.pallas_call(
         edge_kernel,
         out_shape=shape(16, SLOT, 128),
-        in_specs=[SM, SM, VM, VM, ANY],
+        in_specs=[VM, VM, VM, ANY],
         out_specs=ANY,
-        input_output_aliases={4: 0},
+        input_output_aliases={3: 0},
         scratch_shapes=[
             pltpu.VMEM((128, 128), F32),
-            pltpu.VMEM((SLOT, 128), F32),
-            pltpu.SemaphoreType.DMA,
+            pltpu.VMEM((128, 128), F32),
+            pltpu.VMEM((2, SLOT, 128), F32),
+            pltpu.SemaphoreType.DMA((2,)),
         ],
         compiler_params=params(8),
         name="edges",
-    )(side, courant, edge, halo, mine)
+    )(info, edge, halo, mine)
 
 
 def make_tables(where, order, kernels):
@@ -456,9 +456,10 @@
 def local(distribution, collision_order, collision_blocks, kernels):
     v = lax.axis_index("vel")
     rising = v >= 8
-    x = 2 * v + lax.iota(jnp.int32, 2)
-    courant = jnp.abs(COURANT_MAX * (2.0 * x.astype(F32) - (NV - 1)) / (NV - 1))
-    side = jnp.where(rising, -1, 1).astype(jnp.int32)[None]
+    row = lax.broadcasted_iota(jnp.int32, (24, 128), 0)
+    x = (2 * v + (row >= 16)).astype(F32)
+    courant = jnp.abs(COURANT_MAX * (2.0 * x - (NV - 1)) / (NV - 1))
+    info = jnp.where(row < 8, jnp.where(rising, 1.0, -1.0), courant)
     pairs = []
     for s in range(16):
         for u in range(16):
@@ -466,9 +467,9 @@
             if 0 <= to < 16:
                 pairs.append((s * 16 + u, to * 16 + u))
     send = jnp.where(rising, distribution[62:64], distribution[0:2])
-    mine, edge = transport(side, courant, distribution)
+    mine, edge = transport(info, distribution)
     halo = lax.ppermute(send, ("space", "vel"), pairs)
-    mine = edges(side, courant, edge, halo, mine)
+    mine = edges(info, edge, halo, mine)
     where = jnp.stack([v.astype(jnp.int32), collision_blocks[0]])
     tables = make_tables(where, collision_order, kernels)
     cells = exchange(mine, THERE)

time: 43.7 us -> 42.9 us (0.982)
  the two profiles are of different devices: /device:TPU:1 before, /device:TPU:96 now
where the time goes in v4:
time: 42.9 us; the launch traced here: 42.5 us
  blocking collectives  14.7 us (34%)
  starting transfers between devices  11.9 us (28%)
  Pallas kernels  8.73 us (20%)
  waiting for transfers between devices  3.76 us (9%)
  local copies, waits for them, and re-layouts  1.63 us (4%)
  other arithmetic  1.05 us (2%)
  between operations  0.75 us (2%)
    all_to_all x1, blocking collectives, exchange(): lax.all_to_all(slots, 'vel', split_axis=0, concat_axis=0, tiled=True, axi...  14.7 us
    all_to_all x1, starting transfers between devices, exchange(): lax.all_to_all(slots, 'vel', split_axis=0, concat_axis=0, tiled=True, axi...  10 us
    all_to_all x1, waiting for transfers between devices, exchange(): lax.all_to_all(slots, 'vel', split_axis=0, concat_axis=0, tiled=True, axi...  3.76 us
    pallas_call x1, Pallas kernels, collide(): pl.pallas_call(collide_kernel, out_shape=shape(16, SLOT, 128), in_specs=[...  3.63 us
    pallas_call x1, Pallas kernels, make_tables(): pl.pallas_call(tables_kernel, out_shape=[shape(576, 128), shape(8, KERN,...  2.41 us
    ppermute x1, starting transfers between devices, local(): halo = lax.ppermute(send, ('space', 'vel'), pairs)  1.92 us
    unnamed x8, local copies, waits for them, and re-layouts  1.63 us
    pallas_call x1, Pallas kernels, transport(): pl.pallas_call(transport_kernel, out_shape=[shape(16, SLOT, 128), shape(1...  1.14 us
  transfers between devices with their start and end apart: 2, of which 1 were waited for; matrix products, arithmetic and copies ran while one was open for 0% of the time, Pallas kernels for 8%

profile of v4, /device:TPU:96, one launch (start us, length us, event | category | flops | bytes accessed | tf_op | source)
XLA Modules:
  0.0 42.5 jit_solution(5658900068702244793)
XLA Ops:
  0.0 0.9 %slice_select_fusion = f32[2,2048]{1,0:T(2,128)S(1)} fusion(f32[64,2048]{1,0:T(8,128)} %dist_ref.1, pred[]{:T(512)S(6)} %ge.10), kind=kLoop, calls=%fused_computation | loop fusion | flops 4096 | bytes 49153 | tf_op jit(solution)/shard_map/jit(_where)/select_n | solution.py:469
  0.9 1.9 %collective-permute-start = (f32[2,2048]{1,0:T(2,128)S(1)}, f32[2,2048]{1,0:T(2,128)S(1)}, u32[]{:S(2)}, u32[]{:S(2)}) collective-permute-start(f32[2,2048]{1,0:T(2,128)S(1)} %slice_select_fusion), channel_id=1, source_target_pairs={{8,24},{9,25},{10,26},{11,27},{12,28},{13,29},{14,30},{15,31},{16,... | collective-permute-start | bytes 49160 | tf_op jit(solution)/shard_map/ppermute | solution.py:471
  2.9 0.1 broadcast_select_fusion.info_ref
  2.9 0.0 copy-start.1
  2.9 1.0 %copy-done.1 = f32[64,2048]{1,0:T(8,128)S(1)} copy-done((f32[64,2048]{1,0:T(8,128)S(1)}, f32[64,2048]{1,0:T(8,128)}, u32[]{:S(2)}) %copy-start.1) | copy-done | bytes 524312
  4.0 1.1 %transport.1 = (f32[16,64,128]{2,1,0:T(8,128)}, f32[192,128]{1,0:T(8,128)S(1)}) custom-call(f32[24,128]{1,0:T(8,128)S(1)} %broadcast_select_fusion.info_ref, f32[64,2048]{1,0:T(8,128)S(1)} %copy-done.1), custom_call_target="tpu_custom_call" | custom-call | flops 4000000 | bytes 1048576 | tf_op jit(solution)/shard_map/transport/pallas_call | solution.py:361
  5.1 0.0 collective-permute-done.halo_ref
  5.1 0.0 copy-start
  5.1 0.7 %edges.1 = f32[16,64,128]{2,1,0:T(8,128)} custom-call(f32[24,128]{1,0:T(8,128)S(1)} %broadcast_select_fusion.info_ref, f32[192,128]{1,0:T(8,128)S(1)} %get-tuple-element.10.edge_ref, f32[2,2048]{1,0:T(2,128)S(1)} %collective-permute-done.halo_ref, f32[16,64,128]{2,1,0:T(8,128)} %get-tuple-element.11._), custom_call_target="tpu_custom_call", output_to_operand_aliasing={{}: (3, {})} | custom-call | tf_op jit(solution)/shard_map/edges/pallas_call | solution.py:378
  5.8 0.0 copy-start.2
  5.8 10.0 %all-to-all-start = ((f32[16,64,128]{2,1,0:T(8,128)}), f32[16,64,128]{2,1,0:T(8,128)S(1)}, u32[]{:S(2)}, u32[]{:S(2)}) async-start(f32[16,64,128]{2,1,0:T(8,128)} %edges.1), calls=%async_computation | async-start | bytes 1048576 | tf_op jit(solution)/shard_map/all_to_all | solution.py:451
  16.5 0.0 copy-start.3
  16.5 0.1 pad_add_fusion.where_ref
  16.6 0.0 copy-done
  16.6 0.0 copy-done.2
  16.6 0.6 %copy-done.3 = s32[1,64]{1,0:T(1,128)S(1)} copy-done((s32[1,64]{1,0:T(1,128)S(1)}, s32[1,64]{1,0:T(1,128)}, u32[]{:S(2)}) %copy-start.3) | copy-done | bytes 280
  17.2 2.4 %tables.1 = (f32[576,128]{1,0:T(8,128)S(1)}, f32[8,5,32,128]{3,2,1,0:T(8,128)S(1)}, f32[8,128]{1,0:T(8,128)S(1)}) custom-call(s32[2]{0:T(128)S(1)} %pad_add_fusion.where_ref, s32[1,64]{1,0:T(1,128)S(1)} %copy-done.3, f32[5,32768]{1,0:T(8,128)S(1)} %copy-done, f32[832,128]{1,0:T(8,128)S(1)} %copy-done.2), custom_call_target="tpu_custom_call" | custom-call | flops 8000000 | bytes 4194304 | tf_op jit(solution)/shard_map/tables/pallas_call | solution.py:397
  19.6 3.8 %all-to-all-done.x_ref = f32[16,64,128]{2,1,0:T(8,128)S(1)} async-done(((f32[16,64,128]{2,1,0:T(8,128)}), f32[16,64,128]{2,1,0:T(8,128)S(1)}, u32[]{:S(2)}, u32[]{:S(2)}) %all-to-all-start) | async-done | bytes 524320 | tf_op jit(solution)/shard_map/all_to_all | solution.py:451
  23.3 3.6 %collide.1 = f32[16,64,128]{2,1,0:T(8,128)S(1)} custom-call(f32[16,64,128]{2,1,0:T(8,128)S(1)} %all-to-all-done.x_ref, f32[576,128]{1,0:T(8,128)S(1)} %get-tuple-element.12.base_ref, f32[8,5,32,128]{3,2,1,0:T(8,128)S(1)} %get-tuple-element.13.ks_ref, f32[8,128]{1,0:T(8,128)S(1)} %get-tuple-element.14.mask_ref), custom_call_target="tpu_custom_call" | custom-call | tf_op jit(solution)/shard_map/collide/pallas_call | solution.py:414
  27.0 14.7 %all_to_all.10 = f32[16,64,128]{2,1,0:T(8,128)S(1)} all-to-all(f32[16,64,128]{2,1,0:T(8,128)S(1)} %collide.1), channel_id=1, replica_groups={{10,15,5,0,11,14,4,1,9,12,6,3,8,13,7,2},{26,31,21,16,27,30,20,17,25,28,..., dimensions={0} | all-to-all | bytes 1048576 | tf_op jit(solution)/shard_map/all_to_all | solution.py:451
  41.7 0.9 %place.1 = f32[64,2048]{1,0:T(8,128)} custom-call(f32[1024,128]{1,0:T(8,128)S(1)} %bitcast.2), custom_call_target="tpu_custom_call" | custom-call | tf_op jit(solution)/shard_map/place/pallas_call | solution.py:439
  (2 shorter events, 0.0 us)
Async XLA Ops:
  0.9 4.2 %collective-permute-start = (f32[2,2048]{1,0:T(2,128)S(1)}, f32[2,2048]{1,0:T(2,128)S(1)}, u32[]{:S(2)}, u32[]{:S(2)}) collective-permute-start(f32[2,2048]{1,0:T(2,128)S(1)} %slice_select_fusion), channel_id=1, source_target_pairs={{8,24},{9,25},{10,26},{11,27},{12,28},{13,29},{14,30},{15,31},{16,... | collective-permute-start | bytes 49160 | tf_op jit(solution)/shard_map/ppermute | solution.py:471
  2.9 1.0 %copy-start.1 = (f32[64,2048]{1,0:T(8,128)S(1)}, f32[64,2048]{1,0:T(8,128)}, u32[]{:S(2)}) copy-start(f32[64,2048]{1,0:T(8,128)} %dist_ref.1) | copy-start | bytes 1572868
  5.1 11.5 %copy-start = (f32[5,32768]{1,0:T(8,128)S(1)}, f32[5,32768]{1,0:T(8,128)}, u32[]{:S(2)}) copy-start(f32[5,32768]{1,0:T(8,128)} %kern_ref.1) | copy-start | bytes 1966084
  5.8 10.8 %copy-start.2 = (f32[832,128]{1,0:T(8,128)S(1)}, f32[832,128]{1,0:T(8,128)}, u32[]{:S(2)}) copy-start(f32[832,128]{1,0:T(8,128)} %constant.26.clone.const_ref) | copy-start | bytes 1277956
  5.8 17.5 %all-to-all-start = ((f32[16,64,128]{2,1,0:T(8,128)}), f32[16,64,128]{2,1,0:T(8,128)S(1)}, u32[]{:S(2)}, u32[]{:S(2)}) async-start(f32[16,64,128]{2,1,0:T(8,128)} %edges.1), calls=%async_computation | async-start | bytes 1048576 | tf_op jit(solution)/shard_map/all_to_all | solution.py:451
  16.5 0.7 %copy-start.3 = (s32[1,64]{1,0:T(1,128)S(1)}, s32[1,64]{1,0:T(1,128)}, u32[]{:S(2)}) copy-start(s32[1,64]{1,0:T(1,128)} %order_ref.1) | copy-start | bytes 772
